TPU v7x, 32 devices: a whole 2x2x4 slice. The times are simulated.
32 devices in a mesh: blk: 8 (over z, y), off: 4 (over x, core).
Axes of the slice: x: 2, y: 2, z: 4, core: 2. Of those that a mesh axis runs over, the one named last changes fastest.
Arguments:
- orbitals: bfloat16 [8, 48, 2304], P('blk'), may hold values from -1.5 to 1.5
Outputs:
- exchange: float32 [8, 48, 2304], P('blk', 'off')
All inputs are finite; a program needn't handle non-finite values.
Results may differ from a plain program's by a relative error of at most 0.00055.
Values may be sent and summed in bfloat16 or wider, within the bound.
No kernel may reach another device: no remote copies, remote signals or barrier semaphores. Data moves between devices by JAX's collectives and lax.ppermute only.
A program may use at most 64 MiB of HBM per device.

v0:
```python
import functools
import math

import jax
import jax.numpy as jnp
import numpy as np
from jax import lax
from jax.experimental import pallas as pl
from jax.experimental.pallas import tpu as pltpu
from jax.sharding import PartitionSpec as P


cell_edge = 59.0
screen_rate = 0.106
lanes = 128
together_blocks = 2
half = lanes // 2


def signed_points(grid_edge):
    points = np.arange(grid_edge)
    return np.where(points > grid_edge // 2, points - grid_edge, points)


def real_basis(grid_edge):
    points = np.arange(grid_edge)
    angles = 2.0 * np.pi / grid_edge * (points[:, None] * points[None, :] % grid_edge)
    rows = np.where(points[:, None] <= grid_edge // 2, np.cos(angles), np.sin(angles))
    single = (points == 0) | (2 * points == grid_edge)
    return rows * np.sqrt(np.where(single, 1.0, 2.0) / grid_edge)[:, None]


def in_two(values):
    high = values.astype(jnp.bfloat16)
    low = (values - high.astype(np.float64)).astype(jnp.bfloat16)
    return high, low


def left_table(matrix):
    high, low = in_two(matrix)
    return np.concatenate([high, high, low], axis=1)


def right_table(matrix, start_in, start_out):
    edge = matrix.shape[0]
    both = np.zeros((lanes, lanes))
    both[:edge, :edge] = matrix
    both[start_in : start_in + edge, start_out : start_out + edge] = matrix
    high, low = in_two(both)
    return np.block([[high, low], [high, np.zeros_like(low)]])


def screened_kernel(grid_edge):
    signed = signed_points(grid_edge)
    row = np.zeros(lanes, np.int32)
    row[:grid_edge] = signed**2
    row[half : half + grid_edge] = signed**2
    pair = np.where(np.arange(lanes) < half, signed[0::2, None] ** 2, signed[1::2, None] ** 2) + row
    squared = jnp.asarray(pair, jnp.int32)[:, None, :] + jnp.asarray(signed**2, jnp.int32)[None, :, None]
    wave_sq = squared.astype(jnp.float32) * jnp.float32((2.0 * math.pi / cell_edge) ** 2)
    safe_sq = jnp.where(squared == 0, jnp.float32(1.0), wave_sq)
    screened = 4.0 * math.pi * -jnp.expm1(-safe_sq / (4.0 * screen_rate**2)) / safe_sq
    return jnp.where(squared == 0, jnp.float32(math.pi / screen_rate**2), screened)


def split(values):
    high = values.astype(jnp.bfloat16)
    low = (values - high.astype(jnp.float32)).astype(jnp.bfloat16)
    return high, low


def dot(left, right):
    return jnp.dot(left, right, preferred_element_type=jnp.float32)


def rows_products(table, slabs):
    done = []
    for first in range(0, len(slabs), 2):
        columns = []
        for slab in slabs[first : first + 2]:
            high, low = split(slab)
            columns.append(jnp.concatenate([high, low, high], axis=0))
        product = dot(table, jnp.concatenate(columns, axis=1))
        done += [product[:, k * lanes : (k + 1) * lanes] for k in range(len(columns))]
    return done


def lanes_product(slabs, table):
    high, low = split(jnp.concatenate(slabs, axis=0))
    return dot(jnp.concatenate([high, low], axis=1), table)


def lanes_result(product, count):
    edge = product.shape[0] // count
    product = product[:, :lanes] + product[:, lanes:]
    return [product[k * edge : (k + 1) * edge] for k in range(count)]


def in_steps(count, *steps):
    held = [{} for _ in steps]
    for time in range(count + len(steps) - 1):
        for n, step in enumerate(steps):
            item = time - n
            if 0 <= item < count:
                given = (held[n - 1].pop(item),) if n else ()
                held[n][item] = step(item, *given)


def pair_kernel(grid_edge, slots, has_prior, last, *refs):
    refs = list(refs)
    order_ref, home_ref, other_ref, kernel_ref = refs[:4]
    left_first_ref, left_fwd_ref, left_back_ref, left_last_ref, right_fwd_ref, right_back_ref = refs[4:10]
    prior_ref = refs[10] if has_prior else None
    outs = refs[10 + has_prior : -2 - last]
    work, back = refs[-2 - last], refs[-1 - last]
    result = refs[-1] if last else outs[0]

    line = 2 * grid_edge
    group = lanes // math.gcd(lanes, line)
    tiles = group * line // lanes
    pitch = work.shape[0] // (grid_edge // 2)
    planes = grid_edge // slots
    row_tiles = grid_edge * grid_edge // lanes
    lane = lax.broadcasted_iota(jnp.int32, (grid_edge, lanes), 1)
    together = together_blocks if grid_edge % (2 * together_blocks) == 0 else 1
    in_first = lax.broadcasted_iota(jnp.int32, (grid_edge // 2, lanes), 1) < half

    def tiles_of(ref, block):
        first = block * tiles
        return [
            ref[:, (first + t) * lanes : (first + t + 1) * lanes].astype(jnp.float32)
            for t in range(tiles)
        ]

    def turn(values, amount):
        amount %= lanes
        return pltpu.roll(values, amount, 1) if amount else values

    def first_lanes(block):
        dense = [a * b for a, b in zip(tiles_of(home_ref, block), tiles_of(other_ref, block))]
        slabs = []
        for k in range(group):
            tile, offset = divmod(k * line, lanes)
            slab = dense[tile]
            if offset + line > lanes:
                slab = jnp.where(lane >= offset, slab, dense[tile + 1])
            slabs.append(turn(slab, -offset))
        return lanes_product(slabs, right_fwd_ref[...])

    def first_rows(block, product):
        return rows_products(left_first_ref[...], lanes_result(product, group))

    def first_store(block, slabs):
        for k, slab in enumerate(slabs):
            work[pl.ds((block * group + k) * pitch, grid_edge), :] = slab

    in_steps(grid_edge // 2 // group, first_lanes, first_rows, first_store)

    def rows_of(block):
        start = 2 * block * together
        return [
            [pl.ds(start + 2 * k + d, grid_edge // 2, stride=pitch) for d in range(2)]
            for k in range(together)
        ]

    def middle_forward(block):
        slabs = []
        for pair in rows_of(block):
            even, odd = (work[r, :] for r in pair)
            top = jnp.where(in_first, even, turn(odd, half))
            bottom = jnp.where(in_first, turn(even, half), odd)
            slabs.append(jnp.concatenate([top, bottom], axis=0))
        return rows_products(left_fwd_ref[...], slabs)

    def middle_back(block, slabs):
        slabs = [slab * kernel_ref[block * together + k] for k, slab in enumerate(slabs)]
        return rows_products(left_back_ref[...], slabs)

    def middle_store(block, slabs):
        for (row_even, row_odd), slab in zip(rows_of(block), slabs):
            top, bottom = slab[: grid_edge // 2], slab[grid_edge // 2 :]
            back[row_even, :] = jnp.where(in_first, top, turn(bottom, half))
            back[row_odd, :] = jnp.where(in_first, turn(top, half), bottom)

    in_steps(grid_edge // 2 // together, middle_forward, middle_back, middle_store)

    def last_rows(block):
        slabs = [back[pl.ds((block * group + k) * pitch, grid_edge), :] for k in range(group)]
        return rows_products(left_last_ref[...], slabs)

    def last_lanes(block, slabs):
        return lanes_product(slabs, right_back_ref[...])

    def last_store(block, product):
        slabs = [turn(slab, k * line) for k, slab in enumerate(lanes_result(product, group))]
        other = tiles_of(other_ref, block)
        for t in range(tiles):
            sources = range(t * lanes // line, ((t + 1) * lanes - 1) // line + 1)
            dense = slabs[sources[0]]
            for k in sources[1:]:
                dense = jnp.where(lane >= k * line - t * lanes, slabs[k], dense)
            total = -0.25 * (dense * other[t])
            rows = pl.ds(block * tiles + t, planes, stride=row_tiles)
            for p in range(slots):
                result[order_ref[p], rows, :] = total[p * planes : (p + 1) * planes]

    in_steps(grid_edge // 2 // group, last_rows, last_lanes, last_store)

    if last:
        for k in range(slots):
            terms = result[k]
            if has_prior:
                terms += prior_ref[k]
            outs[k % 2][k // 2] = terms
    elif has_prior:
        result[...] += prior_ref[...]


def pair_terms(order, home, other, kernel, prior, last):
    grid_edge, plane_size = home.shape
    slots = order.shape[0]
    basis = real_basis(grid_edge)
    mixed = np.concatenate([np.arange(0, grid_edge, 2), np.arange(1, grid_edge, 2)])
    tables = (
        left_table(basis),
        left_table(basis[:, mixed]),
        left_table(basis.T[mixed]),
        left_table(basis.T),
        right_table(basis.T, grid_edge, half),
        right_table(basis, half, grid_edge),
    )
    slot_rows = grid_edge // slots * plane_size // lanes
    pitch = -(-grid_edge // 8) * 8 + 4
    whole = jax.ShapeDtypeStruct((slots, slot_rows, lanes), jnp.float32)
    part = jax.ShapeDtypeStruct((slots // 2, slot_rows, lanes), jnp.float32)
    vmem = pl.BlockSpec(memory_space=pltpu.VMEM)
    operands = [order, home, other, kernel, *(jnp.asarray(t) for t in tables)]
    operands += [] if prior is None else [prior]
    scratch = [pltpu.VMEM((grid_edge // 2 * pitch, lanes), jnp.float32)] * 2
    scratch += [pltpu.VMEM(whole.shape, jnp.float32)] if last else []
    return pl.pallas_call(
        functools.partial(pair_kernel, grid_edge, slots, prior is not None, last),
        out_shape=(part, part) if last else whole,
        in_specs=[pl.BlockSpec(memory_space=pltpu.SMEM)] + [vmem] * (len(operands) - 1),
        out_specs=(vmem, vmem) if last else vmem,
        scratch_shapes=scratch,
        compiler_params=pltpu.CompilerParams(vmem_limit_bytes=32 * 1024 * 1024),
        cost_estimate=pl.CostEstimate(flops=10**9, bytes_accessed=2 * 10**6, transcendentals=0),
    )(*operands)


def fetch(block, cycle_size, groups):
    across = groups + groups // 2
    routes = ([], [])
    for source in range(cycle_size):
        inner = 4 * source // cycle_size in (1, 2)
        for g in range(groups):
            near = sum(groups >> bit + 1 for bit in range(groups.bit_length() - 1) if g >> bit & 1)
            for turn, mask in enumerate((near ^ across, near) if inner else (near, near ^ across)):
                routes[turn].append((source * groups + g, (source ^ mask) * groups + g))
    first = lax.ppermute(block, ("blk", "off"), routes[0])
    second = lax.ppermute(block, ("blk", "off"), routes[1])
    return first, second


def scattered_sum(near, far, groups):
    bit = 1
    while True:
        arrived = lax.ppermute(far, "off", [(g, g ^ bit) for g in range(groups)])
        near = near + arrived
        bit *= 2
        if bit == groups:
            return near[0]
        near, far = near[0::2], near[1::2]


def on_device(orbitals):
    band_count, grid_edge, plane_size = orbitals.shape
    cycle_size, groups = lax.axis_size("blk"), lax.axis_size("off")
    if cycle_size != 2 * groups or groups & (groups - 1) or groups < 2 or grid_edge > half:
        raise ValueError("unsupported mesh")
    me = lax.axis_index("off")
    first, second = fetch(orbitals, cycle_size, groups)
    kernel = screened_kernel(grid_edge)
    order = jnp.arange(groups, dtype=jnp.int32) ^ me
    rows = []
    for home in orbitals:
        others = [*first, *second]
        terms = None
        for other in others[:-1]:
            terms = pair_terms(order, home, other, kernel, terms, False)
        near, far = pair_terms(order, home, others[-1], kernel, terms, True)
        rows.append(scattered_sum(near, far, groups))
    return jnp.stack(rows).reshape(band_count, grid_edge // groups, plane_size)


def solution(mesh):
    return jax.shard_map(
        on_device,
        mesh=mesh,
        in_specs=(P("blk", None, None),),
        out_specs=P("blk", "off", None),
        check_vma=False,
    )
```

profile of v0, /device:TPU:22, one launch (start us, length us, event | category | flops | bytes accessed | tf_op | source)
XLA Modules:
  0.0 29.2 jit_solution(2904646766138385211)
XLA Ops:
  0.0 0.0 copy-start.7
  0.0 0.0 copy-start.8
  0.0 0.0 copy-start.1
  0.0 0.0 copy-start.2
  0.0 0.0 copy-start.3
  0.0 0.0 copy-start.4
  0.0 0.0 copy-start.5
  0.1 0.0 copy-start.6
  0.1 0.0 copy-start
  0.1 2.4 %collective-permute-start.1 = (bf16[1,48,2304]{2,1,0:T(8,128)(2,1)}, bf16[1,48,2304]{2,1,0:T(8,128)(2,1)S(1)}, u32[]{:S(2)}, u32[]{:S(2)}) collective-permute-start(bf16[1,48,2304]{2,1,0:T(8,128)(2,1)} %param.15), channel_id=1, source_target_pairs={{0,0},{1,9},{2,6},{3,15},{4,4},{5,13},{6,2},{7,11},{8,16},{9,25},{... | collective-permute-start | bytes 663560 | tf_op jit(solution)/shard_map/ppermute | solution.py:261
  2.5 3.4 %collective-permute-start = (bf16[1,48,2304]{2,1,0:T(8,128)(2,1)}, bf16[1,48,2304]{2,1,0:T(8,128)(2,1)S(1)}, u32[]{:S(2)}, u32[]{:S(2)}) collective-permute-start(bf16[1,48,2304]{2,1,0:T(8,128)(2,1)} %param.15), channel_id=1, source_target_pairs={{0,24},{1,17},{2,30},{3,23},{4,28},{5,21},{6,26},{7,19},{8,8},{9,1... | collective-permute-start | bytes 663560 | tf_op jit(solution)/shard_map/ppermute | solution.py:262
  6.0 0.0 copy-done.7
  6.0 0.0 copy-done.8
  6.0 0.4 %fusion.refs_3_ = f32[24,48,128]{2,1,0:T(8,128)S(1)} fusion(s32[48]{0:T(128)S(1)} %copy-done.8, s32[24,128]{1,0:T(8,128)S(1)} %copy-done.7), kind=kLoop, calls=%fused_computation.2 | loop fusion | flops 1622016 | bytes 602304 | tf_op jit(solution)/shard_map/jit(_where)/select_n | solution.py:63
  6.4 10.1 %collective-permute-done.1 = bf16[1,48,2304]{2,1,0:T(8,128)(2,1)S(1)} collective-permute-done((bf16[1,48,2304]{2,1,0:T(8,128)(2,1)}, bf16[1,48,2304]{2,1,0:T(8,128)(2,1)S(1)}, u32[]{:S(2)}, u32[]{:S(2)}) %collective-permute-start.1) | collective-permute-done | bytes 221216 | tf_op jit(solution)/shard_map/ppermute | solution.py:261
  16.5 0.0 copy-done.1
  16.5 0.0 copy-done.2
  16.5 0.0 copy-done.3
  16.5 0.0 copy-done.4
  16.5 0.0 copy-done.5
  16.5 0.0 copy-done.6
  16.6 0.0 copy-done
  16.6 2.6 %shard_map.145.refs_10_ = f32[4,216,128]{2,1,0:T(8,128)S(1)} custom-call(s32[4]{0:T(128)S(1)} %iota_xor_fusion.refs_0_, bf16[48,2304]{1,0:T(8,128)(2,1)S(1)} %bitcast.4, bf16[48,2304]{1,0:T(8,128)(2,1)S(1)} %bitcast.7, f32[24,48,128]{2,1,0:T(8,128)S(1)} %fusion.refs_3_, bf16[48,144]{1,0:T(8,128)(2,1)S(1)} %copy-done.6, bf16[48,144]{1,0:T(8,128)(2,1)S(1)} %copy-done.5, ...), custom_call_target="tpu_custom_call" | custom-call | flops 1000000000 | bytes 2000000 | tf_op jit(solution)/shard_map/pallas_call | solution.py:241
  19.1 0.0 collective-permute-done
  19.2 2.6 %shard_map.146 = (f32[2,216,128]{2,1,0:T(8,128)S(1)}, f32[2,216,128]{2,1,0:T(8,128)S(1)}) custom-call(s32[4]{0:T(128)S(1)} %iota_xor_fusion.refs_0_, bf16[48,2304]{1,0:T(8,128)(2,1)S(1)} %bitcast.5, bf16[48,2304]{1,0:T(8,128)(2,1)S(1)} %bitcast.6, f32[24,48,128]{2,1,0:T(8,128)S(1)} %fusion.refs_3_, bf16[48,144]{1,0:T(8,128)(2,1)S(1)} %copy-done.6, ...), custom_call_target="tpu_custom_call" | custom-call | flops 1000000000 | bytes 2000000 | tf_op jit(solution)/shard_map/pallas_call | solution.py:241
  21.8 0.1 collective-permute-start.2
  21.9 1.5 %collective-permute-done.2 = f32[2,216,128]{2,1,0:T(8,128)S(1)} collective-permute-done((f32[2,216,128]{2,1,0:T(8,128)S(1)}, f32[2,216,128]{2,1,0:T(8,128)S(1)}, u32[]{:S(2)}, u32[]{:S(2)}) %collective-permute-start.2) | collective-permute-done | bytes 221216 | tf_op jit(solution)/shard_map/ppermute | solution.py:269
  23.4 0.1 collective-permute-start.3
  23.4 5.1 %collective-permute-done.3 = f32[1,216,128]{2,1,0:T(8,128)S(1)} collective-permute-done((f32[1,216,128]{2,1,0:T(8,128)S(1)}, f32[1,216,128]{2,1,0:T(8,128)S(1)}, u32[]{:S(2)}, u32[]{:S(2)}) %collective-permute-start.3) | collective-permute-done | bytes 110624 | tf_op jit(solution)/shard_map/ppermute | solution.py:269
  28.5 0.7 %slice_add_fusion = f32[1,216,128]{2,1,0:T(8,128)} fusion(f32[1,216,128]{2,1,0:T(8,128)S(1)} %collective-permute-done.3, f32[2,216,128]{2,1,0:T(8,128)S(1)} %add.22), kind=kLoop, calls=%fused_computation.11 | loop fusion | flops 27648 | bytes 331776 | tf_op jit(solution)/shard_map/add | solution.py:270
  (3 shorter events, 0.0 us)
Async XLA Ops:
  0.0 6.0 %copy-start.7 = (s32[24,128]{1,0:T(8,128)S(1)}, s32[24,128]{1,0:T(8,128)}, u32[]{:S(2)}) copy-start(s32[24,128]{1,0:T(8,128)} %constant.33.clone) | copy-start | bytes 36868
  0.0 6.0 %copy-start.8 = (s32[48]{0:T(128)S(1)}, s32[48]{0:T(128)}, u32[]{:S(2)}) copy-start(s32[48]{0:T(128)} %constant.34.clone) | copy-start | bytes 580
  0.0 16.5 %copy-start.1 = (bf16[256,256]{1,0:T(8,128)(2,1)S(1)}, bf16[256,256]{1,0:T(8,128)(2,1)}, u32[]{:S(2)}) copy-start(bf16[256,256]{1,0:T(8,128)(2,1)} %constant.40.clone.refs_9_) | copy-start | bytes 393220
  0.0 16.5 %copy-start.2 = (bf16[256,256]{1,0:T(8,128)(2,1)S(1)}, bf16[256,256]{1,0:T(8,128)(2,1)}, u32[]{:S(2)}) copy-start(bf16[256,256]{1,0:T(8,128)(2,1)} %constant.39.clone.refs_8_) | copy-start | bytes 393220
  0.0 16.5 %copy-start.3 = (bf16[48,144]{1,0:T(8,128)(2,1)S(1)}, bf16[48,144]{1,0:T(8,128)(2,1)}, u32[]{:S(2)}) copy-start(bf16[48,144]{1,0:T(8,128)(2,1)} %constant.38.clone.refs_7_) | copy-start | bytes 41476
  0.0 16.5 %copy-start.4 = (bf16[48,144]{1,0:T(8,128)(2,1)S(1)}, bf16[48,144]{1,0:T(8,128)(2,1)}, u32[]{:S(2)}) copy-start(bf16[48,144]{1,0:T(8,128)(2,1)} %constant.37.clone.refs_6_) | copy-start | bytes 41476
  0.0 16.5 %copy-start.5 = (bf16[48,144]{1,0:T(8,128)(2,1)S(1)}, bf16[48,144]{1,0:T(8,128)(2,1)}, u32[]{:S(2)}) copy-start(bf16[48,144]{1,0:T(8,128)(2,1)} %constant.36.clone.refs_5_) | copy-start | bytes 41476
  0.1 16.5 %copy-start.6 = (bf16[48,144]{1,0:T(8,128)(2,1)S(1)}, bf16[48,144]{1,0:T(8,128)(2,1)}, u32[]{:S(2)}) copy-start(bf16[48,144]{1,0:T(8,128)(2,1)} %constant.35.clone.refs_4_) | copy-start | bytes 41476
  0.1 16.5 %copy-start = (bf16[1,48,2304]{2,1,0:T(8,128)(2,1)S(1)}, bf16[1,48,2304]{2,1,0:T(8,128)(2,1)}, u32[]{:S(2)}) copy-start(bf16[1,48,2304]{2,1,0:T(8,128)(2,1)} %param.15) | copy-start | bytes 663556
  0.1 16.4 %collective-permute-start.1 = (bf16[1,48,2304]{2,1,0:T(8,128)(2,1)}, bf16[1,48,2304]{2,1,0:T(8,128)(2,1)S(1)}, u32[]{:S(2)}, u32[]{:S(2)}) collective-permute-start(bf16[1,48,2304]{2,1,0:T(8,128)(2,1)} %param.15), channel_id=1, source_target_pairs={{0,0},{1,9},{2,6},{3,15},{4,4},{5,13},{6,2},{7,11},{8,16},{9,25},{... | collective-permute-start | bytes 663560 | tf_op jit(solution)/shard_map/ppermute | solution.py:261
  2.5 16.6 %collective-permute-start = (bf16[1,48,2304]{2,1,0:T(8,128)(2,1)}, bf16[1,48,2304]{2,1,0:T(8,128)(2,1)S(1)}, u32[]{:S(2)}, u32[]{:S(2)}) collective-permute-start(bf16[1,48,2304]{2,1,0:T(8,128)(2,1)} %param.15), channel_id=1, source_target_pairs={{0,24},{1,17},{2,30},{3,23},{4,28},{5,21},{6,26},{7,19},{8,8},{9,1... | collective-permute-start | bytes 663560 | tf_op jit(solution)/shard_map/ppermute | solution.py:262
  21.8 1.5 %collective-permute-start.2 = (f32[2,216,128]{2,1,0:T(8,128)S(1)}, f32[2,216,128]{2,1,0:T(8,128)S(1)}, u32[]{:S(2)}, u32[]{:S(2)}) collective-permute-start(f32[2,216,128]{2,1,0:T(8,128)S(1)} %get-tuple-element.8), channel_id=1, source_target_pairs={{0,1},{1,0},{2,3},{3,2},{4,5},{5,4},{6,7},{7,6},{8,9},{9,8},{10,11... | collective-permute-start | bytes 663560 | tf_op jit(solution)/shard_map/ppermute | solution.py:269
  23.4 5.2 %collective-permute-start.3 = (f32[1,216,128]{2,1,0:T(8,128)S(1)}, f32[1,216,128]{2,1,0:T(8,128)S(1)}, u32[]{:S(2)}, u32[]{:S(2)}) collective-permute-start(f32[1,216,128]{2,1,0:T(8,128)S(1)} %slice.11), channel_id=1, source_target_pairs={{0,2},{1,3},{2,0},{3,1},{4,6},{5,7},{6,4},{7,5},{8,10},{9,11},{10,... | collective-permute-start | bytes 331784 | tf_op jit(solution)/shard_map/ppermute | solution.py:269
where the time goes:
time: 29.4 us; the launch traced here: 29.2 us
  waiting for transfers between devices  16.7 us (57%)
  starting transfers between devices  6 us (20%)
  Pallas kernels  5.19 us (18%)
  other arithmetic  1.11 us (4%)
    ppermute x1, waiting for transfers between devices, fetch(): first = lax.ppermute(block, ('blk', 'off'), routes[0])  10.1 us
    ppermute x2, waiting for transfers between devices, scattered_sum(): arrived = lax.ppermute(far, 'off', [(g, g ^ bit) for g in range(groups)])  6.55 us
    pallas_call x2, Pallas kernels, pair_terms(): pl.pallas_call(functools.partial(pair_kernel, grid_edge, slots, prior is...  5.19 us
    ppermute x1, starting transfers between devices, fetch(): second = lax.ppermute(block, ('blk', 'off'), routes[1])  3.43 us
    ppermute x1, starting transfers between devices, fetch(): first = lax.ppermute(block, ('blk', 'off'), routes[0])  2.43 us
    add x2, other arithmetic, scattered_sum(): near = near + arrived  0.69 us
  transfers between devices with their start and end apart: 4, of which 3 were waited for; matrix products, arithmetic and copies ran while one was open for 1% of the time, Pallas kernels for 9%

commit v1 on v0

--- a/solution.py
+++ b/solution.py
@@ -13,7 +13,6 @@
 cell_edge = 59.0
 screen_rate = 0.106
 lanes = 128
-together_blocks = 2
 half = lanes // 2
 
 
@@ -122,7 +121,7 @@
     planes = grid_edge // slots
     row_tiles = grid_edge * grid_edge // lanes
     lane = lax.broadcasted_iota(jnp.int32, (grid_edge, lanes), 1)
-    together = together_blocks if grid_edge % (2 * together_blocks) == 0 else 1
+    together = 2 if grid_edge % 4 == 0 else 1
     in_first = lax.broadcasted_iota(jnp.int32, (grid_edge // 2, lanes), 1) < half
 
     def tiles_of(ref, block):
@@ -250,14 +249,12 @@
 
 
 def fetch(block, cycle_size, groups):
-    across = groups + groups // 2
     routes = ([], [])
     for source in range(cycle_size):
-        inner = 4 * source // cycle_size in (1, 2)
         for g in range(groups):
-            near = sum(groups >> bit + 1 for bit in range(groups.bit_length() - 1) if g >> bit & 1)
-            for turn, mask in enumerate((near ^ across, near) if inner else (near, near ^ across)):
-                routes[turn].append((source * groups + g, (source ^ mask) * groups + g))
+            for route, mask in zip(routes, (g // 2, g // 2 + groups // 2)):
+                mask = cycle_size - 1 - (mask ^ groups // 2) if g % 2 else mask
+                route.append((source * groups + g, (source ^ mask) * groups + g))
     first = lax.ppermute(block, ("blk", "off"), routes[0])
     second = lax.ppermute(block, ("blk", "off"), routes[1])
     return first, second
@@ -289,8 +286,8 @@
         terms = None
         for other in others[:-1]:
             terms = pair_terms(order, home, other, kernel, terms, False)
-        near, far = pair_terms(order, home, others[-1], kernel, terms, True)
-        rows.append(scattered_sum(near, far, groups))
+        own, rest = pair_terms(order, home, others[-1], kernel, terms, True)
+        rows.append(scattered_sum(own, rest, groups))
     return jnp.stack(rows).reshape(band_count, grid_edge // groups, plane_size)
 
 

time: 29.4 us -> 26.2 us (0.89)
  the two profiles are of different devices: /device:TPU:22 before, /device:TPU:0 now
where the time goes in v1:
time: 26.2 us; the launch traced here: 26.1 us
  starting transfers between devices  12 us (46%)
  waiting for transfers between devices  7.54 us (29%)
  Pallas kernels  5.19 us (20%)
  other arithmetic  1.11 us (4%)
    ppermute x2, starting transfers between devices, scattered_sum(): arrived = lax.ppermute(far, 'off', [(g, g ^ bit) for g in range(groups)])  7.22 us
    pallas_call x2, Pallas kernels, pair_terms(): pl.pallas_call(functools.partial(pair_kernel, grid_edge, slots, prior is...  5.19 us
    ppermute x2, waiting for transfers between devices, scattered_sum(): arrived = lax.ppermute(far, 'off', [(g, g ^ bit) for g in range(groups)])  4.7 us
    ppermute x1, starting transfers between devices, fetch(): second = lax.ppermute(block, ('blk', 'off'), routes[1])  3.07 us
    ppermute x1, waiting for transfers between devices, fetch(): second = lax.ppermute(block, ('blk', 'off'), routes[1])  2.84 us
    ppermute x1, starting transfers between devices, fetch(): first = lax.ppermute(block, ('blk', 'off'), routes[0])  1.73 us
    add x2, other arithmetic, scattered_sum(): near = near + arrived  0.69 us
  transfers between devices with their start and end apart: 4, of which 3 were waited for; matrix products, arithmetic and copies ran while one was open for 2% of the time, Pallas kernels for 10%

profile of v1, /device:TPU:0, one launch (start us, length us, event | category | flops | bytes accessed | tf_op | source)
XLA Modules:
  0.0 26.1 jit_solution(10962576813942691363)
XLA Ops:
  0.0 0.0 copy-start.7
  0.0 0.0 copy-start.8
  0.0 0.0 copy-start.1
  0.0 0.0 copy-start.2
  0.0 0.0 copy-start.3
  0.0 0.0 copy-start.4
  0.0 0.0 copy-start.5
  0.0 0.0 copy-start.6
  0.1 0.0 copy-start
  0.1 1.7 %collective-permute-start.1 = (bf16[1,48,2304]{2,1,0:T(8,128)(2,1)}, bf16[1,48,2304]{2,1,0:T(8,128)(2,1)S(1)}, u32[]{:S(2)}, u32[]{:S(2)}) collective-permute-start(bf16[1,48,2304]{2,1,0:T(8,128)(2,1)} %param.15), channel_id=1, source_target_pairs={{0,0},{1,21},{2,6},{3,19},{4,4},{5,17},{6,2},{7,23},{8,8},{9,29},{... | collective-permute-start | bytes 663560 | tf_op jit(solution)/shard_map/ppermute | solution.py:258
  1.8 3.1 %collective-permute-start = (bf16[1,48,2304]{2,1,0:T(8,128)(2,1)}, bf16[1,48,2304]{2,1,0:T(8,128)(2,1)S(1)}, u32[]{:S(2)}, u32[]{:S(2)}) collective-permute-start(bf16[1,48,2304]{2,1,0:T(8,128)(2,1)} %param.15), channel_id=1, source_target_pairs={{0,8},{1,29},{2,14},{3,27},{4,12},{5,25},{6,10},{7,31},{8,0},{9,21... | collective-permute-start | bytes 663560 | tf_op jit(solution)/shard_map/ppermute | solution.py:259
  4.9 0.0 copy-done.7
  4.9 0.0 copy-done.8
  4.9 0.4 %fusion.refs_3_ = f32[24,48,128]{2,1,0:T(8,128)S(1)} fusion(s32[48]{0:T(128)S(1)} %copy-done.8, s32[24,128]{1,0:T(8,128)S(1)} %copy-done.7), kind=kLoop, calls=%fused_computation.2 | loop fusion | flops 1622016 | bytes 602304 | tf_op jit(solution)/shard_map/jit(_where)/select_n | solution.py:62
  5.3 0.0 collective-permute-done.1
  5.3 0.0 copy-done.1
  5.3 0.0 copy-done.2
  5.3 0.0 copy-done.3
  5.3 0.0 copy-done.4
  5.4 0.0 copy-done.5
  5.4 0.0 copy-done.6
  5.4 0.0 copy-done
  5.4 2.6 %shard_map.145.refs_10_ = f32[4,216,128]{2,1,0:T(8,128)S(1)} custom-call(s32[4]{0:T(128)S(1)} %iota_xor_fusion.refs_0_, bf16[48,2304]{1,0:T(8,128)(2,1)S(1)} %bitcast.4, bf16[48,2304]{1,0:T(8,128)(2,1)S(1)} %bitcast.7, f32[24,48,128]{2,1,0:T(8,128)S(1)} %fusion.refs_3_, bf16[48,144]{1,0:T(8,128)(2,1)S(1)} %copy-done.6, bf16[48,144]{1,0:T(8,128)(2,1)S(1)} %copy-done.5, ...), custom_call_target="tpu_custom_call" | custom-call | flops 1000000000 | bytes 2000000 | tf_op jit(solution)/shard_map/pallas_call | solution.py:240
  8.0 2.8 %collective-permute-done = bf16[1,48,2304]{2,1,0:T(8,128)(2,1)S(1)} collective-permute-done((bf16[1,48,2304]{2,1,0:T(8,128)(2,1)}, bf16[1,48,2304]{2,1,0:T(8,128)(2,1)S(1)}, u32[]{:S(2)}, u32[]{:S(2)}) %collective-permute-start) | collective-permute-done | bytes 221216 | tf_op jit(solution)/shard_map/ppermute | solution.py:259
  10.8 2.6 %shard_map.146 = (f32[2,216,128]{2,1,0:T(8,128)S(1)}, f32[2,216,128]{2,1,0:T(8,128)S(1)}) custom-call(s32[4]{0:T(128)S(1)} %iota_xor_fusion.refs_0_, bf16[48,2304]{1,0:T(8,128)(2,1)S(1)} %bitcast.5, bf16[48,2304]{1,0:T(8,128)(2,1)S(1)} %bitcast.6, f32[24,48,128]{2,1,0:T(8,128)S(1)} %fusion.refs_3_, bf16[48,144]{1,0:T(8,128)(2,1)S(1)} %copy-done.6, ...), custom_call_target="tpu_custom_call" | custom-call | flops 1000000000 | bytes 2000000 | tf_op jit(solution)/shard_map/pallas_call | solution.py:240
  13.4 5.3 %collective-permute-start.2 = (f32[2,216,128]{2,1,0:T(8,128)S(1)}, f32[2,216,128]{2,1,0:T(8,128)S(1)}, u32[]{:S(2)}, u32[]{:S(2)}) collective-permute-start(f32[2,216,128]{2,1,0:T(8,128)S(1)} %get-tuple-element.8), channel_id=1, source_target_pairs={{0,1},{1,0},{2,3},{3,2},{4,5},{5,4},{6,7},{7,6},{8,9},{9,8},{10,11... | collective-permute-start | bytes 663560 | tf_op jit(solution)/shard_map/ppermute | solution.py:266
  18.7 1.1 %collective-permute-done.2 = f32[2,216,128]{2,1,0:T(8,128)S(1)} collective-permute-done((f32[2,216,128]{2,1,0:T(8,128)S(1)}, f32[2,216,128]{2,1,0:T(8,128)S(1)}, u32[]{:S(2)}, u32[]{:S(2)}) %collective-permute-start.2) | collective-permute-done | bytes 221216 | tf_op jit(solution)/shard_map/ppermute | solution.py:266
  19.9 1.9 %collective-permute-start.3 = (f32[1,216,128]{2,1,0:T(8,128)S(1)}, f32[1,216,128]{2,1,0:T(8,128)S(1)}, u32[]{:S(2)}, u32[]{:S(2)}) collective-permute-start(f32[1,216,128]{2,1,0:T(8,128)S(1)} %slice.11), channel_id=1, source_target_pairs={{0,2},{1,3},{2,0},{3,1},{4,6},{5,7},{6,4},{7,5},{8,10},{9,11},{10,... | collective-permute-start | bytes 331784 | tf_op jit(solution)/shard_map/ppermute | solution.py:266
  21.8 3.6 %collective-permute-done.3 = f32[1,216,128]{2,1,0:T(8,128)S(1)} collective-permute-done((f32[1,216,128]{2,1,0:T(8,128)S(1)}, f32[1,216,128]{2,1,0:T(8,128)S(1)}, u32[]{:S(2)}, u32[]{:S(2)}) %collective-permute-start.3) | collective-permute-done | bytes 110624 | tf_op jit(solution)/shard_map/ppermute | solution.py:266
  25.4 0.7 %slice_add_fusion = f32[1,216,128]{2,1,0:T(8,128)} fusion(f32[1,216,128]{2,1,0:T(8,128)S(1)} %collective-permute-done.3, f32[2,216,128]{2,1,0:T(8,128)S(1)} %add.22), kind=kLoop, calls=%fused_computation.11 | loop fusion | flops 27648 | bytes 331776 | tf_op jit(solution)/shard_map/add | solution.py:267
  (3 shorter events, 0.0 us)
Async XLA Ops:
  0.0 4.9 %copy-start.7 = (s32[24,128]{1,0:T(8,128)S(1)}, s32[24,128]{1,0:T(8,128)}, u32[]{:S(2)}) copy-start(s32[24,128]{1,0:T(8,128)} %constant.33.clone) | copy-start | bytes 36868
  0.0 4.9 %copy-start.8 = (s32[48]{0:T(128)S(1)}, s32[48]{0:T(128)}, u32[]{:S(2)}) copy-start(s32[48]{0:T(128)} %constant.34.clone) | copy-start | bytes 580
  0.0 5.3 %copy-start.1 = (bf16[256,256]{1,0:T(8,128)(2,1)S(1)}, bf16[256,256]{1,0:T(8,128)(2,1)}, u32[]{:S(2)}) copy-start(bf16[256,256]{1,0:T(8,128)(2,1)} %constant.40.clone.refs_9_) | copy-start | bytes 393220
  0.0 5.3 %copy-start.2 = (bf16[256,256]{1,0:T(8,128)(2,1)S(1)}, bf16[256,256]{1,0:T(8,128)(2,1)}, u32[]{:S(2)}) copy-start(bf16[256,256]{1,0:T(8,128)(2,1)} %constant.39.clone.refs_8_) | copy-start | bytes 393220
  0.0 5.3 %copy-start.3 = (bf16[48,144]{1,0:T(8,128)(2,1)S(1)}, bf16[48,144]{1,0:T(8,128)(2,1)}, u32[]{:S(2)}) copy-start(bf16[48,144]{1,0:T(8,128)(2,1)} %constant.38.clone.refs_7_) | copy-start | bytes 41476
  0.0 5.3 %copy-start.4 = (bf16[48,144]{1,0:T(8,128)(2,1)S(1)}, bf16[48,144]{1,0:T(8,128)(2,1)}, u32[]{:S(2)}) copy-start(bf16[48,144]{1,0:T(8,128)(2,1)} %constant.37.clone.refs_6_) | copy-start | bytes 41476
  0.0 5.3 %copy-start.5 = (bf16[48,144]{1,0:T(8,128)(2,1)S(1)}, bf16[48,144]{1,0:T(8,128)(2,1)}, u32[]{:S(2)}) copy-start(bf16[48,144]{1,0:T(8,128)(2,1)} %constant.36.clone.refs_5_) | copy-start | bytes 41476
  0.0 5.3 %copy-start.6 = (bf16[48,144]{1,0:T(8,128)(2,1)S(1)}, bf16[48,144]{1,0:T(8,128)(2,1)}, u32[]{:S(2)}) copy-start(bf16[48,144]{1,0:T(8,128)(2,1)} %constant.35.clone.refs_4_) | copy-start | bytes 41476
  0.1 5.3 %copy-start = (bf16[1,48,2304]{2,1,0:T(8,128)(2,1)S(1)}, bf16[1,48,2304]{2,1,0:T(8,128)(2,1)}, u32[]{:S(2)}) copy-start(bf16[1,48,2304]{2,1,0:T(8,128)(2,1)} %param.15) | copy-start | bytes 663556
  0.1 5.2 %collective-permute-start.1 = (bf16[1,48,2304]{2,1,0:T(8,128)(2,1)}, bf16[1,48,2304]{2,1,0:T(8,128)(2,1)S(1)}, u32[]{:S(2)}, u32[]{:S(2)}) collective-permute-start(bf16[1,48,2304]{2,1,0:T(8,128)(2,1)} %param.15), channel_id=1, source_target_pairs={{0,0},{1,21},{2,6},{3,19},{4,4},{5,17},{6,2},{7,23},{8,8},{9,29},{... | collective-permute-start | bytes 663560 | tf_op jit(solution)/shard_map/ppermute | solution.py:258
  1.8 9.0 %collective-permute-start = (bf16[1,48,2304]{2,1,0:T(8,128)(2,1)}, bf16[1,48,2304]{2,1,0:T(8,128)(2,1)S(1)}, u32[]{:S(2)}, u32[]{:S(2)}) collective-permute-start(bf16[1,48,2304]{2,1,0:T(8,128)(2,1)} %param.15), channel_id=1, source_target_pairs={{0,8},{1,29},{2,14},{3,27},{4,12},{5,25},{6,10},{7,31},{8,0},{9,21... | collective-permute-start | bytes 663560 | tf_op jit(solution)/shard_map/ppermute | solution.py:259
  13.4 6.4 %collective-permute-start.2 = (f32[2,216,128]{2,1,0:T(8,128)S(1)}, f32[2,216,128]{2,1,0:T(8,128)S(1)}, u32[]{:S(2)}, u32[]{:S(2)}) collective-permute-start(f32[2,216,128]{2,1,0:T(8,128)S(1)} %get-tuple-element.8), channel_id=1, source_target_pairs={{0,1},{1,0},{2,3},{3,2},{4,5},{5,4},{6,7},{7,6},{8,9},{9,8},{10,11... | collective-permute-start | bytes 663560 | tf_op jit(solution)/shard_map/ppermute | solution.py:266
  19.9 5.5 %collective-permute-start.3 = (f32[1,216,128]{2,1,0:T(8,128)S(1)}, f32[1,216,128]{2,1,0:T(8,128)S(1)}, u32[]{:S(2)}, u32[]{:S(2)}) collective-permute-start(f32[1,216,128]{2,1,0:T(8,128)S(1)} %slice.11), channel_id=1, source_target_pairs={{0,2},{1,3},{2,0},{3,1},{4,6},{5,7},{6,4},{7,5},{8,10},{9,11},{10,... | collective-permute-start | bytes 331784 | tf_op jit(solution)/shard_map/ppermute | solution.py:266

commit v2 on v1

--- a/solution.py
+++ b/solution.py
@@ -107,13 +107,14 @@
 
 def pair_kernel(grid_edge, slots, has_prior, last, *refs):
     refs = list(refs)
-    order_ref, home_ref, other_ref, kernel_ref = refs[:4]
-    left_first_ref, left_fwd_ref, left_back_ref, left_last_ref, right_fwd_ref, right_back_ref = refs[4:10]
-    prior_ref = refs[10] if has_prior else None
-    outs = refs[10 + has_prior : -2 - last]
+    home_ref, other_ref, kernel_ref = refs[:3]
+    left_first_ref, left_fwd_ref, left_back_ref, left_last_ref, right_fwd_ref, right_back_ref = refs[3:9]
+    prior_ref = refs[9] if has_prior else None
+    outs = refs[9 + has_prior : -2 - last]
     work, back = refs[-2 - last], refs[-1 - last]
     result = refs[-1] if last else outs[0]
 
+    me = lax.axis_index("off")
     line = 2 * grid_edge
     group = lanes // math.gcd(lanes, line)
     tiles = group * line // lanes
@@ -201,7 +202,7 @@
             total = -0.25 * (dense * other[t])
             rows = pl.ds(block * tiles + t, planes, stride=row_tiles)
             for p in range(slots):
-                result[order_ref[p], rows, :] = total[p * planes : (p + 1) * planes]
+                result[me ^ p, rows, :] = total[p * planes : (p + 1) * planes]
 
     in_steps(grid_edge // 2 // group, last_rows, last_lanes, last_store)
 
@@ -215,9 +216,8 @@
         result[...] += prior_ref[...]
 
 
-def pair_terms(order, home, other, kernel, prior, last):
+def pair_terms(slots, home, other, kernel, prior, last):
     grid_edge, plane_size = home.shape
-    slots = order.shape[0]
     basis = real_basis(grid_edge)
     mixed = np.concatenate([np.arange(0, grid_edge, 2), np.arange(1, grid_edge, 2)])
     tables = (
@@ -233,14 +233,14 @@
     whole = jax.ShapeDtypeStruct((slots, slot_rows, lanes), jnp.float32)
     part = jax.ShapeDtypeStruct((slots // 2, slot_rows, lanes), jnp.float32)
     vmem = pl.BlockSpec(memory_space=pltpu.VMEM)
-    operands = [order, home, other, kernel, *(jnp.asarray(t) for t in tables)]
+    operands = [home, other, kernel, *(jnp.asarray(t) for t in tables)]
     operands += [] if prior is None else [prior]
     scratch = [pltpu.VMEM((grid_edge // 2 * pitch, lanes), jnp.float32)] * 2
     scratch += [pltpu.VMEM(whole.shape, jnp.float32)] if last else []
     return pl.pallas_call(
         functools.partial(pair_kernel, grid_edge, slots, prior is not None, last),
         out_shape=(part, part) if last else whole,
-        in_specs=[pl.BlockSpec(memory_space=pltpu.SMEM)] + [vmem] * (len(operands) - 1),
+        in_specs=[vmem] * len(operands),
         out_specs=(vmem, vmem) if last else vmem,
         scratch_shapes=scratch,
         compiler_params=pltpu.CompilerParams(vmem_limit_bytes=32 * 1024 * 1024),
@@ -276,17 +276,15 @@
     cycle_size, groups = lax.axis_size("blk"), lax.axis_size("off")
     if cycle_size != 2 * groups or groups & (groups - 1) or groups < 2 or grid_edge > half:
         raise ValueError("unsupported mesh")
-    me = lax.axis_index("off")
     first, second = fetch(orbitals, cycle_size, groups)
     kernel = screened_kernel(grid_edge)
-    order = jnp.arange(groups, dtype=jnp.int32) ^ me
     rows = []
     for home in orbitals:
         others = [*first, *second]
         terms = None
         for other in others[:-1]:
-            terms = pair_terms(order, home, other, kernel, terms, False)
-        own, rest = pair_terms(order, home, others[-1], kernel, terms, True)
+            terms = pair_terms(groups, home, other, kernel, terms, False)
+        own, rest = pair_terms(groups, home, others[-1], kernel, terms, True)
         rows.append(scattered_sum(own, rest, groups))
     return jnp.stack(rows).reshape(band_count, grid_edge // groups, plane_size)
 

time: 26.2 us -> 25.6 us (0.977)
  Pallas kernels: 5.19 us -> 4.1 us
  other arithmetic: 1.11 us -> 1.81 us
    pallas_call x2, Pallas kernels: 5.19 us -> 4.1 us  [pair_terms(): pl.pallas_call(functools.partial(pair_kernel, grid_edge, slots, prior is...]
    select_n x1, other arithmetic: 0.41 us -> 1.12 us  [screened_kernel(): jnp.where(squared == 0, jnp.float32(math.pi / screen_rate ** 2), screened)]
  transfers between devices with their start and end apart: 4 -> 4, of which waited for: 3 -> 3; matrix products, arithmetic and copies ran while one was open for 2% -> 4% of each run, Pallas kernels for 10% -> 8%
where the time goes in v2:
time: 25.6 us; the launch traced here: 25.4 us
  starting transfers between devices  11.8 us (46%)
  waiting for transfers between devices  7.44 us (29%)
  Pallas kernels  4.1 us (16%)
  other arithmetic  1.81 us (7%)
    ppermute x2, starting transfers between devices, scattered_sum(): arrived = lax.ppermute(far, 'off', [(g, g ^ bit) for g in range(groups)])  7.05 us
    ppermute x2, waiting for transfers between devices, scattered_sum(): arrived = lax.ppermute(far, 'off', [(g, g ^ bit) for g in range(groups)])  4.74 us
    pallas_call x2, Pallas kernels, pair_terms(): pl.pallas_call(functools.partial(pair_kernel, grid_edge, slots, prior is...  4.1 us
    ppermute x1, starting transfers between devices, fetch(): second = lax.ppermute(block, ('blk', 'off'), routes[1])  3.07 us
    ppermute x1, waiting for transfers between devices, fetch(): second = lax.ppermute(block, ('blk', 'off'), routes[1])  2.7 us
    ppermute x1, starting transfers between devices, fetch(): first = lax.ppermute(block, ('blk', 'off'), routes[0])  1.73 us
    select_n x1, other arithmetic, screened_kernel(): jnp.where(squared == 0, jnp.float32(math.pi / screen_rate ** 2), screened)  1.12 us
    add x2, other arithmetic, scattered_sum(): near = near + arrived  0.69 us
  transfers between devices with their start and end apart: 4, of which 3 were waited for; matrix products, arithmetic and copies ran while one was open for 4% of the time, Pallas kernels for 8%

profile of v2, /device:TPU:0, one launch (start us, length us, event | category | flops | bytes accessed | tf_op | source)
XLA Modules:
  0.0 25.4 jit_solution(11200742566099645134)
XLA Ops:
  0.0 0.0 copy-start.7
  0.0 0.0 copy-start.1
  0.0 0.0 copy-start.2
  0.0 0.0 copy-start.3
  0.0 0.0 copy-start.4
  0.0 0.0 copy-start.5
  0.0 0.0 copy-start.6
  0.0 0.0 copy-start
  0.1 1.7 %collective-permute-start.1 = (bf16[1,48,2304]{2,1,0:T(8,128)(2,1)}, bf16[1,48,2304]{2,1,0:T(8,128)(2,1)S(1)}, u32[]{:S(2)}, u32[]{:S(2)}) collective-permute-start(bf16[1,48,2304]{2,1,0:T(8,128)(2,1)} %param.15), channel_id=1, source_target_pairs={{0,0},{1,21},{2,6},{3,19},{4,4},{5,17},{6,2},{7,23},{8,8},{9,29},{... | collective-permute-start | bytes 663560 | tf_op jit(solution)/shard_map/ppermute | solution.py:258
  1.8 3.1 %collective-permute-start = (bf16[1,48,2304]{2,1,0:T(8,128)(2,1)}, bf16[1,48,2304]{2,1,0:T(8,128)(2,1)S(1)}, u32[]{:S(2)}, u32[]{:S(2)}) collective-permute-start(bf16[1,48,2304]{2,1,0:T(8,128)(2,1)} %param.15), channel_id=1, source_target_pairs={{0,8},{1,29},{2,14},{3,27},{4,12},{5,25},{6,10},{7,31},{8,0},{9,21... | collective-permute-start | bytes 663560 | tf_op jit(solution)/shard_map/ppermute | solution.py:259
  4.8 0.0 copy-done.7
  4.9 1.1 %fusion.refs_2_ = f32[24,48,128]{2,1,0:T(8,128)S(1)} fusion(s32[48]{0:T(128)S(1)} %copy-done.7, s32[24,128]{1,0:T(8,128)} %constant.29.clone), kind=kLoop, calls=%fused_computation.2 | loop fusion | flops 1622016 | bytes 602304 | tf_op jit(solution)/shard_map/jit(_where)/select_n | solution.py:62
  6.0 0.0 collective-permute-done.1
  6.0 0.0 copy-done.1
  6.0 0.0 copy-done.2
  6.0 0.0 copy-done.3
  6.0 0.0 copy-done.4
  6.0 0.0 copy-done.5
  6.0 0.0 copy-done.6
  6.0 0.0 copy-done
  6.1 2.0 %shard_map.145.refs_9_ = f32[4,216,128]{2,1,0:T(8,128)S(1)} custom-call(bf16[48,2304]{1,0:T(8,128)(2,1)S(1)} %bitcast.4, bf16[48,2304]{1,0:T(8,128)(2,1)S(1)} %bitcast.7, f32[24,48,128]{2,1,0:T(8,128)S(1)} %fusion.refs_2_, bf16[48,144]{1,0:T(8,128)(2,1)S(1)} %copy-done.6, bf16[48,144]{1,0:T(8,128)(2,1)S(1)} %copy-done.5, bf16[48,144]{1,0:T(8,128)(2,1)S(1)} %copy-done.4, ...), custom_call_target="tpu_custom_call" | custom-call | flops 1000000000 | bytes 2000000 | tf_op jit(solution)/shard_map/pallas_call | solution.py:240
  8.1 2.7 %collective-permute-done = bf16[1,48,2304]{2,1,0:T(8,128)(2,1)S(1)} collective-permute-done((bf16[1,48,2304]{2,1,0:T(8,128)(2,1)}, bf16[1,48,2304]{2,1,0:T(8,128)(2,1)S(1)}, u32[]{:S(2)}, u32[]{:S(2)}) %collective-permute-start) | collective-permute-done | bytes 221216 | tf_op jit(solution)/shard_map/ppermute | solution.py:259
  10.8 2.1 %shard_map.146 = (f32[2,216,128]{2,1,0:T(8,128)S(1)}, f32[2,216,128]{2,1,0:T(8,128)S(1)}) custom-call(bf16[48,2304]{1,0:T(8,128)(2,1)S(1)} %bitcast.5, bf16[48,2304]{1,0:T(8,128)(2,1)S(1)} %bitcast.6, f32[24,48,128]{2,1,0:T(8,128)S(1)} %fusion.refs_2_, bf16[48,144]{1,0:T(8,128)(2,1)S(1)} %copy-done.6, bf16[48,144]{1,0:T(8,128)(2,1)S(1)} %copy-done.5, ...), custom_call_target="tpu_custom_call" | custom-call | flops 1000000000 | bytes 2000000 | tf_op jit(solution)/shard_map/pallas_call | solution.py:240
  12.9 5.3 %collective-permute-start.2 = (f32[2,216,128]{2,1,0:T(8,128)S(1)}, f32[2,216,128]{2,1,0:T(8,128)S(1)}, u32[]{:S(2)}, u32[]{:S(2)}) collective-permute-start(f32[2,216,128]{2,1,0:T(8,128)S(1)} %get-tuple-element.8), channel_id=1, source_target_pairs={{0,1},{1,0},{2,3},{3,2},{4,5},{5,4},{6,7},{7,6},{8,9},{9,8},{10,11... | collective-permute-start | bytes 663560 | tf_op jit(solution)/shard_map/ppermute | solution.py:266
  18.1 1.1 %collective-permute-done.2 = f32[2,216,128]{2,1,0:T(8,128)S(1)} collective-permute-done((f32[2,216,128]{2,1,0:T(8,128)S(1)}, f32[2,216,128]{2,1,0:T(8,128)S(1)}, u32[]{:S(2)}, u32[]{:S(2)}) %collective-permute-start.2) | collective-permute-done | bytes 221216 | tf_op jit(solution)/shard_map/ppermute | solution.py:266
  19.3 1.8 %collective-permute-start.3 = (f32[1,216,128]{2,1,0:T(8,128)S(1)}, f32[1,216,128]{2,1,0:T(8,128)S(1)}, u32[]{:S(2)}, u32[]{:S(2)}) collective-permute-start(f32[1,216,128]{2,1,0:T(8,128)S(1)} %slice.11), channel_id=1, source_target_pairs={{0,2},{1,3},{2,0},{3,1},{4,6},{5,7},{6,4},{7,5},{8,10},{9,11},{10,... | collective-permute-start | bytes 331784 | tf_op jit(solution)/shard_map/ppermute | solution.py:266
  21.1 3.6 %collective-permute-done.3 = f32[1,216,128]{2,1,0:T(8,128)S(1)} collective-permute-done((f32[1,216,128]{2,1,0:T(8,128)S(1)}, f32[1,216,128]{2,1,0:T(8,128)S(1)}, u32[]{:S(2)}, u32[]{:S(2)}) %collective-permute-start.3) | collective-permute-done | bytes 110624 | tf_op jit(solution)/shard_map/ppermute | solution.py:266
  24.7 0.7 %slice_add_fusion = f32[1,216,128]{2,1,0:T(8,128)} fusion(f32[1,216,128]{2,1,0:T(8,128)S(1)} %collective-permute-done.3, f32[2,216,128]{2,1,0:T(8,128)S(1)} %add.22), kind=kLoop, calls=%fused_computation.11 | loop fusion | flops 27648 | bytes 331776 | tf_op jit(solution)/shard_map/add | solution.py:267
  (2 shorter events, 0.0 us)
Async XLA Ops:
  0.0 4.8 %copy-start.7 = (s32[48]{0:T(128)S(1)}, s32[48]{0:T(128)}, u32[]{:S(2)}) copy-start(s32[48]{0:T(128)} %constant.30.clone) | copy-start | bytes 580
  0.0 6.0 %copy-start.1 = (bf16[256,256]{1,0:T(8,128)(2,1)S(1)}, bf16[256,256]{1,0:T(8,128)(2,1)}, u32[]{:S(2)}) copy-start(bf16[256,256]{1,0:T(8,128)(2,1)} %constant.36.clone.refs_8_) | copy-start | bytes 393220
  0.0 6.0 %copy-start.2 = (bf16[256,256]{1,0:T(8,128)(2,1)S(1)}, bf16[256,256]{1,0:T(8,128)(2,1)}, u32[]{:S(2)}) copy-start(bf16[256,256]{1,0:T(8,128)(2,1)} %constant.35.clone.refs_7_) | copy-start | bytes 393220
  0.0 6.0 %copy-start.3 = (bf16[48,144]{1,0:T(8,128)(2,1)S(1)}, bf16[48,144]{1,0:T(8,128)(2,1)}, u32[]{:S(2)}) copy-start(bf16[48,144]{1,0:T(8,128)(2,1)} %constant.34.clone.refs_6_) | copy-start | bytes 41476
  0.0 6.0 %copy-start.4 = (bf16[48,144]{1,0:T(8,128)(2,1)S(1)}, bf16[48,144]{1,0:T(8,128)(2,1)}, u32[]{:S(2)}) copy-start(bf16[48,144]{1,0:T(8,128)(2,1)} %constant.33.clone.refs_5_) | copy-start | bytes 41476
  0.0 6.0 %copy-start.5 = (bf16[48,144]{1,0:T(8,128)(2,1)S(1)}, bf16[48,144]{1,0:T(8,128)(2,1)}, u32[]{:S(2)}) copy-start(bf16[48,144]{1,0:T(8,128)(2,1)} %constant.32.clone.refs_4_) | copy-start | bytes 41476
  0.0 6.0 %copy-start.6 = (bf16[48,144]{1,0:T(8,128)(2,1)S(1)}, bf16[48,144]{1,0:T(8,128)(2,1)}, u32[]{:S(2)}) copy-start(bf16[48,144]{1,0:T(8,128)(2,1)} %constant.31.clone.refs_3_) | copy-start | bytes 41476
  0.0 6.0 %copy-start = (bf16[1,48,2304]{2,1,0:T(8,128)(2,1)S(1)}, bf16[1,48,2304]{2,1,0:T(8,128)(2,1)}, u32[]{:S(2)}) copy-start(bf16[1,48,2304]{2,1,0:T(8,128)(2,1)} %param.15) | copy-start | bytes 663556
  0.1 5.9 %collective-permute-start.1 = (bf16[1,48,2304]{2,1,0:T(8,128)(2,1)}, bf16[1,48,2304]{2,1,0:T(8,128)(2,1)S(1)}, u32[]{:S(2)}, u32[]{:S(2)}) collective-permute-start(bf16[1,48,2304]{2,1,0:T(8,128)(2,1)} %param.15), channel_id=1, source_target_pairs={{0,0},{1,21},{2,6},{3,19},{4,4},{5,17},{6,2},{7,23},{8,8},{9,29},{... | collective-permute-start | bytes 663560 | tf_op jit(solution)/shard_map/ppermute | solution.py:258
  1.8 9.0 %collective-permute-start = (bf16[1,48,2304]{2,1,0:T(8,128)(2,1)}, bf16[1,48,2304]{2,1,0:T(8,128)(2,1)S(1)}, u32[]{:S(2)}, u32[]{:S(2)}) collective-permute-start(bf16[1,48,2304]{2,1,0:T(8,128)(2,1)} %param.15), channel_id=1, source_target_pairs={{0,8},{1,29},{2,14},{3,27},{4,12},{5,25},{6,10},{7,31},{8,0},{9,21... | collective-permute-start | bytes 663560 | tf_op jit(solution)/shard_map/ppermute | solution.py:259
  12.9 6.4 %collective-permute-start.2 = (f32[2,216,128]{2,1,0:T(8,128)S(1)}, f32[2,216,128]{2,1,0:T(8,128)S(1)}, u32[]{:S(2)}, u32[]{:S(2)}) collective-permute-start(f32[2,216,128]{2,1,0:T(8,128)S(1)} %get-tuple-element.8), channel_id=1, source_target_pairs={{0,1},{1,0},{2,3},{3,2},{4,5},{5,4},{6,7},{7,6},{8,9},{9,8},{10,11... | collective-permute-start | bytes 663560 | tf_op jit(solution)/shard_map/ppermute | solution.py:266
  19.3 5.4 %collective-permute-start.3 = (f32[1,216,128]{2,1,0:T(8,128)S(1)}, f32[1,216,128]{2,1,0:T(8,128)S(1)}, u32[]{:S(2)}, u32[]{:S(2)}) collective-permute-start(f32[1,216,128]{2,1,0:T(8,128)S(1)} %slice.11), channel_id=1, source_target_pairs={{0,2},{1,3},{2,0},{3,1},{4,6},{5,7},{6,4},{7,5},{8,10},{9,11},{10,... | collective-permute-start | bytes 331784 | tf_op jit(solution)/shard_map/ppermute | solution.py:266

commit v3 on v2

--- a/solution.py
+++ b/solution.py
@@ -95,14 +95,10 @@
     return [product[k * edge : (k + 1) * edge] for k in range(count)]
 
 
-def in_steps(count, *steps):
-    held = [{} for _ in steps]
-    for time in range(count + len(steps) - 1):
-        for n, step in enumerate(steps):
-            item = time - n
-            if 0 <= item < count:
-                given = (held[n - 1].pop(item),) if n else ()
-                held[n][item] = step(item, *given)
+def in_stages(count, *stages):
+    results = [()] * count
+    for stage in stages:
+        results = [(stage(i, *given),) for i, given in enumerate(results)]
 
 
 def pair_kernel(grid_edge, slots, has_prior, last, *refs):
@@ -154,7 +150,7 @@
         for k, slab in enumerate(slabs):
             work[pl.ds((block * group + k) * pitch, grid_edge), :] = slab
 
-    in_steps(grid_edge // 2 // group, first_lanes, first_rows, first_store)
+    in_stages(grid_edge // 2 // group, first_lanes, first_rows, first_store)
 
     def rows_of(block):
         start = 2 * block * together
@@ -182,7 +178,7 @@
             back[row_even, :] = jnp.where(in_first, top, turn(bottom, half))
             back[row_odd, :] = jnp.where(in_first, turn(top, half), bottom)
 
-    in_steps(grid_edge // 2 // together, middle_forward, middle_back, middle_store)
+    in_stages(grid_edge // 2 // together, middle_forward, middle_back, middle_store)
 
     def last_rows(block):
         slabs = [back[pl.ds((block * group + k) * pitch, grid_edge), :] for k in range(group)]
@@ -204,7 +200,7 @@
             for p in range(slots):
                 result[me ^ p, rows, :] = total[p * planes : (p + 1) * planes]
 
-    in_steps(grid_edge // 2 // group, last_rows, last_lanes, last_store)
+    in_stages(grid_edge // 2 // group, last_rows, last_lanes, last_store)
 
     if last:
         for k in range(slots):
@@ -252,8 +248,8 @@
     routes = ([], [])
     for source in range(cycle_size):
         for g in range(groups):
-            for route, mask in zip(routes, (g // 2, g // 2 + groups // 2)):
-                mask = cycle_size - 1 - (mask ^ groups // 2) if g % 2 else mask
+            for route, mask in zip(routes, (g // 2 + groups // 2, g // 2)):
+                mask = cycle_size - 1 - mask if g % 2 else mask
                 route.append((source * groups + g, (source ^ mask) * groups + g))
     first = lax.ppermute(block, ("blk", "off"), routes[0])
     second = lax.ppermute(block, ("blk", "off"), routes[1])

time: 25.6 us -> 23.7 us (0.926)
  starting transfers between devices: 11.8 us -> 8.68 us
  waiting for transfers between devices: 7.44 us -> 9.34 us
  Pallas kernels: 4.1 us -> 3.45 us
    ppermute x1, waiting for transfers between devices: 0.01 us -> 3.24 us  [fetch(): first = lax.ppermute(block, ('blk', 'off'), routes[0])]
    ppermute x2, starting transfers between devices: 7.05 us -> 3.96 us  [scattered_sum(): arrived = lax.ppermute(far, 'off', [(g, g ^ bit) for g in range(groups)])]
    ppermute x1, waiting for transfers between devices: 2.7 us -> 0.01 us  [fetch(): second = lax.ppermute(block, ('blk', 'off'), routes[1])]
    ppermute x1, starting transfers between devices: 3.07 us -> 1.58 us  [fetch(): second = lax.ppermute(block, ('blk', 'off'), routes[1])]
    ppermute x1, starting transfers between devices: 1.73 us -> 3.14 us  [fetch(): first = lax.ppermute(block, ('blk', 'off'), routes[0])]
    ppermute x2, waiting for transfers between devices: 4.74 us -> 6.09 us  [scattered_sum(): arrived = lax.ppermute(far, 'off', [(g, g ^ bit) for g in range(groups)])]
    pallas_call x2, Pallas kernels: 4.1 us -> 3.45 us  [pair_terms(): pl.pallas_call(functools.partial(pair_kernel, grid_edge, slots, prior is...]
  transfers between devices with their start and end apart: 4 -> 4, of which waited for: 3 -> 3; matrix products, arithmetic and copies ran while one was open for 4% -> 5% of each run, Pallas kernels for 8% -> 7%
where the time goes in v3:
time: 23.7 us; the launch traced here: 23.4 us
  waiting for transfers between devices  9.34 us (39%)
  starting transfers between devices  8.68 us (37%)
  Pallas kernels  3.45 us (15%)
  other arithmetic  1.81 us (8%)
    ppermute x2, waiting for transfers between devices, scattered_sum(): arrived = lax.ppermute(far, 'off', [(g, g ^ bit) for g in range(groups)])  6.09 us
    ppermute x2, starting transfers between devices, scattered_sum(): arrived = lax.ppermute(far, 'off', [(g, g ^ bit) for g in range(groups)])  3.96 us
    pallas_call x2, Pallas kernels, pair_terms(): pl.pallas_call(functools.partial(pair_kernel, grid_edge, slots, prior is...  3.45 us
    ppermute x1, waiting for transfers between devices, fetch(): first = lax.ppermute(block, ('blk', 'off'), routes[0])  3.24 us
    ppermute x1, starting transfers between devices, fetch(): first = lax.ppermute(block, ('blk', 'off'), routes[0])  3.14 us
    ppermute x1, starting transfers between devices, fetch(): second = lax.ppermute(block, ('blk', 'off'), routes[1])  1.58 us
    select_n x1, other arithmetic, screened_kernel(): jnp.where(squared == 0, jnp.float32(math.pi / screen_rate ** 2), screened)  1.12 us
    add x2, other arithmetic, scattered_sum(): near = near + arrived  0.69 us
  transfers between devices with their start and end apart: 4, of which 3 were waited for; matrix products, arithmetic and copies ran while one was open for 5% of the time, Pallas kernels for 7%

profile of v3, /device:TPU:0, one launch (start us, length us, event | category | flops | bytes accessed | tf_op | source)
XLA Modules:
  0.0 23.4 jit_solution(11094222000108003369)
XLA Ops:
  0.0 0.0 copy-start.7
  0.0 0.0 copy-start.1
  0.0 0.0 copy-start.2
  0.0 0.0 copy-start.3
  0.0 0.0 copy-start.4
  0.0 0.0 copy-start.5
  0.0 0.0 copy-start.6
  0.0 0.0 copy-start
  0.1 3.1 %collective-permute-start.1 = (bf16[1,48,2304]{2,1,0:T(8,128)(2,1)}, bf16[1,48,2304]{2,1,0:T(8,128)(2,1)S(1)}, u32[]{:S(2)}, u32[]{:S(2)}) collective-permute-start(bf16[1,48,2304]{2,1,0:T(8,128)(2,1)} %param.15), channel_id=1, source_target_pairs={{0,8},{1,21},{2,14},{3,19},{4,12},{5,17},{6,10},{7,23},{8,0},{9,29... | collective-permute-start | bytes 663560 | tf_op jit(solution)/shard_map/ppermute | solution.py:254
  3.2 1.6 %collective-permute-start = (bf16[1,48,2304]{2,1,0:T(8,128)(2,1)}, bf16[1,48,2304]{2,1,0:T(8,128)(2,1)S(1)}, u32[]{:S(2)}, u32[]{:S(2)}) collective-permute-start(bf16[1,48,2304]{2,1,0:T(8,128)(2,1)} %param.15), channel_id=1, source_target_pairs={{0,0},{1,29},{2,6},{3,27},{4,4},{5,25},{6,2},{7,31},{8,8},{9,21},{... | collective-permute-start | bytes 663560 | tf_op jit(solution)/shard_map/ppermute | solution.py:255
  4.8 0.0 copy-done.7
  4.8 1.1 %fusion.refs_2_ = f32[24,48,128]{2,1,0:T(8,128)S(1)} fusion(s32[48]{0:T(128)S(1)} %copy-done.7, s32[24,128]{1,0:T(8,128)} %constant.29.clone), kind=kLoop, calls=%fused_computation.2 | loop fusion | flops 1622016 | bytes 602304 | tf_op jit(solution)/shard_map/jit(_where)/select_n | solution.py:62
  5.9 3.2 %collective-permute-done.1 = bf16[1,48,2304]{2,1,0:T(8,128)(2,1)S(1)} collective-permute-done((bf16[1,48,2304]{2,1,0:T(8,128)(2,1)}, bf16[1,48,2304]{2,1,0:T(8,128)(2,1)S(1)}, u32[]{:S(2)}, u32[]{:S(2)}) %collective-permute-start.1) | collective-permute-done | bytes 221216 | tf_op jit(solution)/shard_map/ppermute | solution.py:254
  9.1 0.0 copy-done.1
  9.1 0.0 copy-done.2
  9.1 0.0 copy-done.3
  9.1 0.0 copy-done.4
  9.2 0.0 copy-done.5
  9.2 0.0 copy-done.6
  9.2 0.0 copy-done
  9.2 1.7 %shard_map.145.refs_9_ = f32[4,216,128]{2,1,0:T(8,128)S(1)} custom-call(bf16[48,2304]{1,0:T(8,128)(2,1)S(1)} %bitcast.4, bf16[48,2304]{1,0:T(8,128)(2,1)S(1)} %bitcast.7, f32[24,48,128]{2,1,0:T(8,128)S(1)} %fusion.refs_2_, bf16[48,144]{1,0:T(8,128)(2,1)S(1)} %copy-done.6, bf16[48,144]{1,0:T(8,128)(2,1)S(1)} %copy-done.5, bf16[48,144]{1,0:T(8,128)(2,1)S(1)} %copy-done.4, ...), custom_call_target="tpu_custom_call" | custom-call | flops 1000000000 | bytes 2000000 | tf_op jit(solution)/shard_map/pallas_call | solution.py:236
  10.9 0.0 collective-permute-done
  10.9 1.8 %shard_map.146 = (f32[2,216,128]{2,1,0:T(8,128)S(1)}, f32[2,216,128]{2,1,0:T(8,128)S(1)}) custom-call(bf16[48,2304]{1,0:T(8,128)(2,1)S(1)} %bitcast.5, bf16[48,2304]{1,0:T(8,128)(2,1)S(1)} %bitcast.6, f32[24,48,128]{2,1,0:T(8,128)S(1)} %fusion.refs_2_, bf16[48,144]{1,0:T(8,128)(2,1)S(1)} %copy-done.6, bf16[48,144]{1,0:T(8,128)(2,1)S(1)} %copy-done.5, ...), custom_call_target="tpu_custom_call" | custom-call | flops 1000000000 | bytes 2000000 | tf_op jit(solution)/shard_map/pallas_call | solution.py:236
  12.7 3.5 %collective-permute-start.2 = (f32[2,216,128]{2,1,0:T(8,128)S(1)}, f32[2,216,128]{2,1,0:T(8,128)S(1)}, u32[]{:S(2)}, u32[]{:S(2)}) collective-permute-start(f32[2,216,128]{2,1,0:T(8,128)S(1)} %get-tuple-element.8), channel_id=1, source_target_pairs={{0,1},{1,0},{2,3},{3,2},{4,5},{5,4},{6,7},{7,6},{8,9},{9,8},{10,11... | collective-permute-start | bytes 663560 | tf_op jit(solution)/shard_map/ppermute | solution.py:262
  16.2 1.1 %collective-permute-done.2 = f32[2,216,128]{2,1,0:T(8,128)S(1)} collective-permute-done((f32[2,216,128]{2,1,0:T(8,128)S(1)}, f32[2,216,128]{2,1,0:T(8,128)S(1)}, u32[]{:S(2)}, u32[]{:S(2)}) %collective-permute-start.2) | collective-permute-done | bytes 221216 | tf_op jit(solution)/shard_map/ppermute | solution.py:262
  17.4 0.4 %collective-permute-start.3 = (f32[1,216,128]{2,1,0:T(8,128)S(1)}, f32[1,216,128]{2,1,0:T(8,128)S(1)}, u32[]{:S(2)}, u32[]{:S(2)}) collective-permute-start(f32[1,216,128]{2,1,0:T(8,128)S(1)} %slice.11), channel_id=1, source_target_pairs={{0,2},{1,3},{2,0},{3,1},{4,6},{5,7},{6,4},{7,5},{8,10},{9,11},{10,... | collective-permute-start | bytes 331784 | tf_op jit(solution)/shard_map/ppermute | solution.py:262
  17.8 5.0 %collective-permute-done.3 = f32[1,216,128]{2,1,0:T(8,128)S(1)} collective-permute-done((f32[1,216,128]{2,1,0:T(8,128)S(1)}, f32[1,216,128]{2,1,0:T(8,128)S(1)}, u32[]{:S(2)}, u32[]{:S(2)}) %collective-permute-start.3) | collective-permute-done | bytes 110624 | tf_op jit(solution)/shard_map/ppermute | solution.py:262
  22.8 0.7 %slice_add_fusion = f32[1,216,128]{2,1,0:T(8,128)} fusion(f32[1,216,128]{2,1,0:T(8,128)S(1)} %collective-permute-done.3, f32[2,216,128]{2,1,0:T(8,128)S(1)} %add.22), kind=kLoop, calls=%fused_computation.11 | loop fusion | flops 27648 | bytes 331776 | tf_op jit(solution)/shard_map/add | solution.py:263
  (2 shorter events, 0.0 us)
Async XLA Ops:
  0.0 4.8 %copy-start.7 = (s32[48]{0:T(128)S(1)}, s32[48]{0:T(128)}, u32[]{:S(2)}) copy-start(s32[48]{0:T(128)} %constant.30.clone) | copy-start | bytes 580
  0.0 9.1 %copy-start.1 = (bf16[256,256]{1,0:T(8,128)(2,1)S(1)}, bf16[256,256]{1,0:T(8,128)(2,1)}, u32[]{:S(2)}) copy-start(bf16[256,256]{1,0:T(8,128)(2,1)} %constant.36.clone.refs_8_) | copy-start | bytes 393220
  0.0 9.1 %copy-start.2 = (bf16[256,256]{1,0:T(8,128)(2,1)S(1)}, bf16[256,256]{1,0:T(8,128)(2,1)}, u32[]{:S(2)}) copy-start(bf16[256,256]{1,0:T(8,128)(2,1)} %constant.35.clone.refs_7_) | copy-start | bytes 393220
  0.0 9.1 %copy-start.3 = (bf16[48,144]{1,0:T(8,128)(2,1)S(1)}, bf16[48,144]{1,0:T(8,128)(2,1)}, u32[]{:S(2)}) copy-start(bf16[48,144]{1,0:T(8,128)(2,1)} %constant.34.clone.refs_6_) | copy-start | bytes 41476
  0.0 9.1 %copy-start.4 = (bf16[48,144]{1,0:T(8,128)(2,1)S(1)}, bf16[48,144]{1,0:T(8,128)(2,1)}, u32[]{:S(2)}) copy-start(bf16[48,144]{1,0:T(8,128)(2,1)} %constant.33.clone.refs_5_) | copy-start | bytes 41476
  0.0 9.1 %copy-start.5 = (bf16[48,144]{1,0:T(8,128)(2,1)S(1)}, bf16[48,144]{1,0:T(8,128)(2,1)}, u32[]{:S(2)}) copy-start(bf16[48,144]{1,0:T(8,128)(2,1)} %constant.32.clone.refs_4_) | copy-start | bytes 41476
  0.0 9.1 %copy-start.6 = (bf16[48,144]{1,0:T(8,128)(2,1)S(1)}, bf16[48,144]{1,0:T(8,128)(2,1)}, u32[]{:S(2)}) copy-start(bf16[48,144]{1,0:T(8,128)(2,1)} %constant.31.clone.refs_3_) | copy-start | bytes 41476
  0.0 9.1 %copy-start = (bf16[1,48,2304]{2,1,0:T(8,128)(2,1)S(1)}, bf16[1,48,2304]{2,1,0:T(8,128)(2,1)}, u32[]{:S(2)}) copy-start(bf16[1,48,2304]{2,1,0:T(8,128)(2,1)} %param.15) | copy-start | bytes 663556
  0.1 9.1 %collective-permute-start.1 = (bf16[1,48,2304]{2,1,0:T(8,128)(2,1)}, bf16[1,48,2304]{2,1,0:T(8,128)(2,1)S(1)}, u32[]{:S(2)}, u32[]{:S(2)}) collective-permute-start(bf16[1,48,2304]{2,1,0:T(8,128)(2,1)} %param.15), channel_id=1, source_target_pairs={{0,8},{1,21},{2,14},{3,19},{4,12},{5,17},{6,10},{7,23},{8,0},{9,29... | collective-permute-start | bytes 663560 | tf_op jit(solution)/shard_map/ppermute | solution.py:254
  3.2 7.7 %collective-permute-start = (bf16[1,48,2304]{2,1,0:T(8,128)(2,1)}, bf16[1,48,2304]{2,1,0:T(8,128)(2,1)S(1)}, u32[]{:S(2)}, u32[]{:S(2)}) collective-permute-start(bf16[1,48,2304]{2,1,0:T(8,128)(2,1)} %param.15), channel_id=1, source_target_pairs={{0,0},{1,29},{2,6},{3,27},{4,4},{5,25},{6,2},{7,31},{8,8},{9,21},{... | collective-permute-start | bytes 663560 | tf_op jit(solution)/shard_map/ppermute | solution.py:255
  12.7 4.7 %collective-permute-start.2 = (f32[2,216,128]{2,1,0:T(8,128)S(1)}, f32[2,216,128]{2,1,0:T(8,128)S(1)}, u32[]{:S(2)}, u32[]{:S(2)}) collective-permute-start(f32[2,216,128]{2,1,0:T(8,128)S(1)} %get-tuple-element.8), channel_id=1, source_target_pairs={{0,1},{1,0},{2,3},{3,2},{4,5},{5,4},{6,7},{7,6},{8,9},{9,8},{10,11... | collective-permute-start | bytes 663560 | tf_op jit(solution)/shard_map/ppermute | solution.py:262
  17.4 5.4 %collective-permute-start.3 = (f32[1,216,128]{2,1,0:T(8,128)S(1)}, f32[1,216,128]{2,1,0:T(8,128)S(1)}, u32[]{:S(2)}, u32[]{:S(2)}) collective-permute-start(f32[1,216,128]{2,1,0:T(8,128)S(1)} %slice.11), channel_id=1, source_target_pairs={{0,2},{1,3},{2,0},{3,1},{4,6},{5,7},{6,4},{7,5},{8,10},{9,11},{10,... | collective-permute-start | bytes 331784 | tf_op jit(solution)/shard_map/ppermute | solution.py:262

commit v4 on v3

--- a/solution.py
+++ b/solution.py
@@ -207,7 +207,7 @@
             terms = result[k]
             if has_prior:
                 terms += prior_ref[k]
-            outs[k % 2][k // 2] = terms
+            outs[k % 4][k // 4] = terms
     elif has_prior:
         result[...] += prior_ref[...]
 
@@ -227,7 +227,7 @@
     slot_rows = grid_edge // slots * plane_size // lanes
     pitch = -(-grid_edge // 8) * 8 + 4
     whole = jax.ShapeDtypeStruct((slots, slot_rows, lanes), jnp.float32)
-    part = jax.ShapeDtypeStruct((slots // 2, slot_rows, lanes), jnp.float32)
+    part = jax.ShapeDtypeStruct((slots // 4, slot_rows, lanes), jnp.float32)
     vmem = pl.BlockSpec(memory_space=pltpu.VMEM)
     operands = [home, other, kernel, *(jnp.asarray(t) for t in tables)]
     operands += [] if prior is None else [prior]
@@ -235,9 +235,9 @@
     scratch += [pltpu.VMEM(whole.shape, jnp.float32)] if last else []
     return pl.pallas_call(
         functools.partial(pair_kernel, grid_edge, slots, prior is not None, last),
-        out_shape=(part, part) if last else whole,
+        out_shape=(part,) * 4 if last else whole,
         in_specs=[vmem] * len(operands),
-        out_specs=(vmem, vmem) if last else vmem,
+        out_specs=(vmem,) * 4 if last else vmem,
         scratch_shapes=scratch,
         compiler_params=pltpu.CompilerParams(vmem_limit_bytes=32 * 1024 * 1024),
         cost_estimate=pl.CostEstimate(flops=10**9, bytes_accessed=2 * 10**6, transcendentals=0),
@@ -248,7 +248,7 @@
     routes = ([], [])
     for source in range(cycle_size):
         for g in range(groups):
-            for route, mask in zip(routes, (g // 2 + groups // 2, g // 2)):
+            for route, mask in zip(routes, (groups - 1 - g // 2, g // 2)):
                 mask = cycle_size - 1 - mask if g % 2 else mask
                 route.append((source * groups + g, (source ^ mask) * groups + g))
     first = lax.ppermute(block, ("blk", "off"), routes[0])
@@ -256,8 +256,12 @@
     return first, second
 
 
-def scattered_sum(near, far, groups):
-    bit = 1
+def scattered_sum(parts, groups):
+    to_neighbour = [(g, g ^ 1) for g in range(groups)]
+    passed_on = lax.ppermute(parts[3], "off", to_neighbour)
+    kept = lax.ppermute(parts[1], "off", to_neighbour)
+    near, far = parts[0] + kept, parts[2] + passed_on
+    bit = 2
     while True:
         arrived = lax.ppermute(far, "off", [(g, g ^ bit) for g in range(groups)])
         near = near + arrived
@@ -270,7 +274,7 @@
 def on_device(orbitals):
     band_count, grid_edge, plane_size = orbitals.shape
     cycle_size, groups = lax.axis_size("blk"), lax.axis_size("off")
-    if cycle_size != 2 * groups or groups & (groups - 1) or groups < 2 or grid_edge > half:
+    if cycle_size != 2 * groups or groups & (groups - 1) or groups < 4 or grid_edge > half:
         raise ValueError("unsupported mesh")
     first, second = fetch(orbitals, cycle_size, groups)
     kernel = screened_kernel(grid_edge)
@@ -280,8 +284,8 @@
         terms = None
         for other in others[:-1]:
             terms = pair_terms(groups, home, other, kernel, terms, False)
-        own, rest = pair_terms(groups, home, others[-1], kernel, terms, True)
-        rows.append(scattered_sum(own, rest, groups))
+        parts = pair_terms(groups, home, others[-1], kernel, terms, True)
+        rows.append(scattered_sum(parts, groups))
     return jnp.stack(rows).reshape(band_count, grid_edge // groups, plane_size)
 
 

time: 23.7 us -> 23.2 us (0.979)
  waiting for transfers between devices: 9.34 us -> 8.15 us
  starting transfers between devices: 8.68 us -> 9.41 us
    ppermute x2 -> x1, starting transfers between devices: 3.96 us -> 1.51 us  [scattered_sum(): arrived = lax.ppermute(far, 'off', [(g, g ^ bit) for g in range(groups)])]
    ppermute x0 -> x2, starting transfers between devices: none -> 2.23 us  [the longest x1 2.15 us: scattered_sum(): passed_on = lax.ppermute(parts[3], 'off', to_neighbour)]
    ppermute x2 -> x1, waiting for transfers between devices: 6.09 us -> 3.87 us  [scattered_sum(): arrived = lax.ppermute(far, 'off', [(g, g ^ bit) for g in range(groups)])]
    ppermute x1, starting transfers between devices: 3.14 us -> 4.09 us  [fetch(): first = lax.ppermute(block, ('blk', 'off'), routes[0])]
    ppermute x0 -> x2, waiting for transfers between devices: none -> 0.88 us  [the longest x1 0.88 us: scattered_sum(): passed_on = lax.ppermute(parts[3], 'off', to_neighbour)]
    add x2 -> x1, other arithmetic: 0.69 us -> 0.66 us  [scattered_sum(): near = near + arrived]
  transfers between devices with their start and end apart: 4 -> 5, of which waited for: 3 -> 3; matrix products, arithmetic and copies ran while one was open for 5% -> 5% of each run, Pallas kernels for 7% -> 7%
where the time goes in v4:
time: 23.2 us; the launch traced here: 22.9 us
  starting transfers between devices  9.41 us (41%)
  waiting for transfers between devices  8.15 us (35%)
  Pallas kernels  3.44 us (15%)
  other arithmetic  1.8 us (8%)
    ppermute x1, starting transfers between devices, fetch(): first = lax.ppermute(block, ('blk', 'off'), routes[0])  4.09 us
    ppermute x1, waiting for transfers between devices, scattered_sum(): arrived = lax.ppermute(far, 'off', [(g, g ^ bit) for g in range(groups)])  3.87 us
    pallas_call x2, Pallas kernels, pair_terms(): pl.pallas_call(functools.partial(pair_kernel, grid_edge, slots, prior is...  3.44 us
    ppermute x1, waiting for transfers between devices, fetch(): first = lax.ppermute(block, ('blk', 'off'), routes[0])  3.39 us
    ppermute x1, starting transfers between devices, scattered_sum(): passed_on = lax.ppermute(parts[3], 'off', to_neighbour)  2.15 us
    ppermute x1, starting transfers between devices, fetch(): second = lax.ppermute(block, ('blk', 'off'), routes[1])  1.58 us
    ppermute x1, starting transfers between devices, scattered_sum(): arrived = lax.ppermute(far, 'off', [(g, g ^ bit) for g in range(groups)])  1.51 us
    select_n x1, other arithmetic, screened_kernel(): jnp.where(squared == 0, jnp.float32(math.pi / screen_rate ** 2), screened)  1.12 us
  transfers between devices with their start and end apart: 5, of which 3 were waited for; matrix products, arithmetic and copies ran while one was open for 5% of the time, Pallas kernels for 7%

profile of v4, /device:TPU:0, one launch (start us, length us, event | category | flops | bytes accessed | tf_op | source)
XLA Modules:
  0.0 22.9 jit_solution(8450515976241158738)
XLA Ops:
  0.0 0.0 copy-start.7
  0.0 0.0 copy-start.1
  0.0 0.0 copy-start.2
  0.0 0.0 copy-start.3
  0.0 0.0 copy-start.4
  0.0 0.0 copy-start.5
  0.0 0.0 copy-start.6
  0.0 0.0 copy-start
  0.1 4.1 %collective-permute-start.1 = (bf16[1,48,2304]{2,1,0:T(8,128)(2,1)}, bf16[1,48,2304]{2,1,0:T(8,128)(2,1)S(1)}, u32[]{:S(2)}, u32[]{:S(2)}) collective-permute-start(bf16[1,48,2304]{2,1,0:T(8,128)(2,1)} %param.15), channel_id=1, source_target_pairs={{0,12},{1,17},{2,10},{3,23},{4,8},{5,21},{6,14},{7,19},{8,4},{9,25... | collective-permute-start | bytes 663560 | tf_op jit(solution)/shard_map/ppermute | solution.py:254
  4.1 1.6 %collective-permute-start = (bf16[1,48,2304]{2,1,0:T(8,128)(2,1)}, bf16[1,48,2304]{2,1,0:T(8,128)(2,1)S(1)}, u32[]{:S(2)}, u32[]{:S(2)}) collective-permute-start(bf16[1,48,2304]{2,1,0:T(8,128)(2,1)} %param.15), channel_id=1, source_target_pairs={{0,0},{1,29},{2,6},{3,27},{4,4},{5,25},{6,2},{7,31},{8,8},{9,21},{... | collective-permute-start | bytes 663560 | tf_op jit(solution)/shard_map/ppermute | solution.py:255
  5.7 0.0 copy-done.7
  5.7 1.1 %fusion.refs_2_ = f32[24,48,128]{2,1,0:T(8,128)S(1)} fusion(s32[48]{0:T(128)S(1)} %copy-done.7, s32[24,128]{1,0:T(8,128)} %constant.29.clone), kind=kLoop, calls=%fused_computation.2 | loop fusion | flops 1622016 | bytes 602304 | tf_op jit(solution)/shard_map/jit(_where)/select_n | solution.py:62
  6.9 3.4 %collective-permute-done.1 = bf16[1,48,2304]{2,1,0:T(8,128)(2,1)S(1)} collective-permute-done((bf16[1,48,2304]{2,1,0:T(8,128)(2,1)}, bf16[1,48,2304]{2,1,0:T(8,128)(2,1)S(1)}, u32[]{:S(2)}, u32[]{:S(2)}) %collective-permute-start.1) | collective-permute-done | bytes 221216 | tf_op jit(solution)/shard_map/ppermute | solution.py:254
  10.2 0.0 copy-done.1
  10.2 0.0 copy-done.2
  10.3 0.0 copy-done.3
  10.3 0.0 copy-done.4
  10.3 0.0 copy-done.5
  10.3 0.0 copy-done.6
  10.3 0.0 copy-done
  10.3 1.7 %shard_map.145.refs_9_ = f32[4,216,128]{2,1,0:T(8,128)S(1)} custom-call(bf16[48,2304]{1,0:T(8,128)(2,1)S(1)} %bitcast.4, bf16[48,2304]{1,0:T(8,128)(2,1)S(1)} %bitcast.7, f32[24,48,128]{2,1,0:T(8,128)S(1)} %fusion.refs_2_, bf16[48,144]{1,0:T(8,128)(2,1)S(1)} %copy-done.6, bf16[48,144]{1,0:T(8,128)(2,1)S(1)} %copy-done.5, bf16[48,144]{1,0:T(8,128)(2,1)S(1)} %copy-done.4, ...), custom_call_target="tpu_custom_call" | custom-call | flops 1000000000 | bytes 2000000 | tf_op jit(solution)/shard_map/pallas_call | solution.py:236
  12.0 0.0 collective-permute-done
  12.0 1.7 %shard_map.146 = (f32[1,216,128]{2,1,0:T(8,128)S(1)}, f32[1,216,128]{2,1,0:T(8,128)S(1)}, f32[1,216,128]{2,1,0:T(8,128)S(1)}, f32[1,216,128]{2,1,0:T(8,128)S(1)}) custom-call(bf16[48,2304]{1,0:T(8,128)(2,1)S(1)} %bitcast.5, bf16[48,2304]{1,0:T(8,128)(2,1)S(1)} %bitcast.6, f32[24,48,128]{2,1,0:T(8,128)S(1)} %fusion.refs_2_, bf16[48,144]{1,0:T(8,128)(2,1)S(1)} %copy-done.6, ...), custom_call_target="tpu_custom_call" | custom-call | flops 1000000000 | bytes 2000000 | tf_op jit(solution)/shard_map/pallas_call | solution.py:236
  13.8 2.1 %collective-permute-start.3 = (f32[1,216,128]{2,1,0:T(8,128)S(1)}, f32[1,216,128]{2,1,0:T(8,128)S(1)}, u32[]{:S(2)}, u32[]{:S(2)}) collective-permute-start(f32[1,216,128]{2,1,0:T(8,128)S(1)} %get-tuple-element.12), channel_id=1, source_target_pairs={{0,1},{1,0},{2,3},{3,2},{4,5},{5,4},{6,7},{7,6},{8,9},{9,8},{10,11... | collective-permute-start | bytes 331784 | tf_op jit(solution)/shard_map/ppermute | solution.py:261
  15.9 0.1 collective-permute-start.2
  16.0 0.9 %collective-permute-done.3 = f32[1,216,128]{2,1,0:T(8,128)S(1)} collective-permute-done((f32[1,216,128]{2,1,0:T(8,128)S(1)}, f32[1,216,128]{2,1,0:T(8,128)S(1)}, u32[]{:S(2)}, u32[]{:S(2)}) %collective-permute-start.3) | collective-permute-done | bytes 110624 | tf_op jit(solution)/shard_map/ppermute | solution.py:261
  16.9 1.5 %collective-permute-start.4 = (f32[1,216,128]{2,1,0:T(8,128)S(1)}, f32[1,216,128]{2,1,0:T(8,128)S(1)}, u32[]{:S(2)}, u32[]{:S(2)}) collective-permute-start(f32[1,216,128]{2,1,0:T(8,128)S(1)} %add.26), channel_id=1, source_target_pairs={{0,2},{1,3},{2,0},{3,1},{4,6},{5,7},{6,4},{7,5},{8,10},{9,11},{10,... | collective-permute-start | bytes 331784 | tf_op jit(solution)/shard_map/ppermute | solution.py:266
  18.4 0.0 collective-permute-done.2
  18.4 3.9 %collective-permute-done.4 = f32[1,216,128]{2,1,0:T(8,128)S(1)} collective-permute-done((f32[1,216,128]{2,1,0:T(8,128)S(1)}, f32[1,216,128]{2,1,0:T(8,128)S(1)}, u32[]{:S(2)}, u32[]{:S(2)}) %collective-permute-start.4) | collective-permute-done | bytes 110624 | tf_op jit(solution)/shard_map/ppermute | solution.py:266
  22.3 0.7 %add_add_fusion = f32[1,216,128]{2,1,0:T(8,128)} fusion(f32[1,216,128]{2,1,0:T(8,128)S(1)} %collective-permute-done.4, f32[1,216,128]{2,1,0:T(8,128)S(1)} %get-tuple-element.9, f32[1,216,128]{2,1,0:T(8,128)S(1)} %collective-permute-done.2), kind=kLoop, calls=%fused_computation.11 | loop fusion | flops 55296 | bytes 442368 | tf_op jit(solution)/shard_map/add | solution.py:267
  (1 shorter events, 0.0 us)
Async XLA Ops:
  0.0 5.7 %copy-start.7 = (s32[48]{0:T(128)S(1)}, s32[48]{0:T(128)}, u32[]{:S(2)}) copy-start(s32[48]{0:T(128)} %constant.30.clone) | copy-start | bytes 580
  0.0 10.2 %copy-start.1 = (bf16[256,256]{1,0:T(8,128)(2,1)S(1)}, bf16[256,256]{1,0:T(8,128)(2,1)}, u32[]{:S(2)}) copy-start(bf16[256,256]{1,0:T(8,128)(2,1)} %constant.36.clone.refs_8_) | copy-start | bytes 393220
  0.0 10.2 %copy-start.2 = (bf16[256,256]{1,0:T(8,128)(2,1)S(1)}, bf16[256,256]{1,0:T(8,128)(2,1)}, u32[]{:S(2)}) copy-start(bf16[256,256]{1,0:T(8,128)(2,1)} %constant.35.clone.refs_7_) | copy-start | bytes 393220
  0.0 10.2 %copy-start.3 = (bf16[48,144]{1,0:T(8,128)(2,1)S(1)}, bf16[48,144]{1,0:T(8,128)(2,1)}, u32[]{:S(2)}) copy-start(bf16[48,144]{1,0:T(8,128)(2,1)} %constant.34.clone.refs_6_) | copy-start | bytes 41476
  0.0 10.3 %copy-start.4 = (bf16[48,144]{1,0:T(8,128)(2,1)S(1)}, bf16[48,144]{1,0:T(8,128)(2,1)}, u32[]{:S(2)}) copy-start(bf16[48,144]{1,0:T(8,128)(2,1)} %constant.33.clone.refs_5_) | copy-start | bytes 41476
  0.0 10.3 %copy-start.5 = (bf16[48,144]{1,0:T(8,128)(2,1)S(1)}, bf16[48,144]{1,0:T(8,128)(2,1)}, u32[]{:S(2)}) copy-start(bf16[48,144]{1,0:T(8,128)(2,1)} %constant.32.clone.refs_4_) | copy-start | bytes 41476
  0.0 10.3 %copy-start.6 = (bf16[48,144]{1,0:T(8,128)(2,1)S(1)}, bf16[48,144]{1,0:T(8,128)(2,1)}, u32[]{:S(2)}) copy-start(bf16[48,144]{1,0:T(8,128)(2,1)} %constant.31.clone.refs_3_) | copy-start | bytes 41476
  0.0 10.2 %copy-start = (bf16[1,48,2304]{2,1,0:T(8,128)(2,1)S(1)}, bf16[1,48,2304]{2,1,0:T(8,128)(2,1)}, u32[]{:S(2)}) copy-start(bf16[1,48,2304]{2,1,0:T(8,128)(2,1)} %param.15) | copy-start | bytes 663556
  0.1 10.2 %collective-permute-start.1 = (bf16[1,48,2304]{2,1,0:T(8,128)(2,1)}, bf16[1,48,2304]{2,1,0:T(8,128)(2,1)S(1)}, u32[]{:S(2)}, u32[]{:S(2)}) collective-permute-start(bf16[1,48,2304]{2,1,0:T(8,128)(2,1)} %param.15), channel_id=1, source_target_pairs={{0,12},{1,17},{2,10},{3,23},{4,8},{5,21},{6,14},{7,19},{8,4},{9,25... | collective-permute-start | bytes 663560 | tf_op jit(solution)/shard_map/ppermute | solution.py:254
  4.1 7.9 %collective-permute-start = (bf16[1,48,2304]{2,1,0:T(8,128)(2,1)}, bf16[1,48,2304]{2,1,0:T(8,128)(2,1)S(1)}, u32[]{:S(2)}, u32[]{:S(2)}) collective-permute-start(bf16[1,48,2304]{2,1,0:T(8,128)(2,1)} %param.15), channel_id=1, source_target_pairs={{0,0},{1,29},{2,6},{3,27},{4,4},{5,25},{6,2},{7,31},{8,8},{9,21},{... | collective-permute-start | bytes 663560 | tf_op jit(solution)/shard_map/ppermute | solution.py:255
  13.8 3.1 %collective-permute-start.3 = (f32[1,216,128]{2,1,0:T(8,128)S(1)}, f32[1,216,128]{2,1,0:T(8,128)S(1)}, u32[]{:S(2)}, u32[]{:S(2)}) collective-permute-start(f32[1,216,128]{2,1,0:T(8,128)S(1)} %get-tuple-element.12), channel_id=1, source_target_pairs={{0,1},{1,0},{2,3},{3,2},{4,5},{5,4},{6,7},{7,6},{8,9},{9,8},{10,11... | collective-permute-start | bytes 331784 | tf_op jit(solution)/shard_map/ppermute | solution.py:261
  15.9 2.5 %collective-permute-start.2 = (f32[1,216,128]{2,1,0:T(8,128)S(1)}, f32[1,216,128]{2,1,0:T(8,128)S(1)}, u32[]{:S(2)}, u32[]{:S(2)}) collective-permute-start(f32[1,216,128]{2,1,0:T(8,128)S(1)} %get-tuple-element.10), channel_id=1, source_target_pairs={{0,1},{1,0},{2,3},{3,2},{4,5},{5,4},{6,7},{7,6},{8,9},{9,8},{10,11... | collective-permute-start | bytes 331784 | tf_op jit(solution)/shard_map/ppermute | solution.py:262
  16.9 5.4 %collective-permute-start.4 = (f32[1,216,128]{2,1,0:T(8,128)S(1)}, f32[1,216,128]{2,1,0:T(8,128)S(1)}, u32[]{:S(2)}, u32[]{:S(2)}) collective-permute-start(f32[1,216,128]{2,1,0:T(8,128)S(1)} %add.26), channel_id=1, source_target_pairs={{0,2},{1,3},{2,0},{3,1},{4,6},{5,7},{6,4},{7,5},{8,10},{9,11},{10,... | collective-permute-start | bytes 331784 | tf_op jit(solution)/shard_map/ppermute | solution.py:266

commit v5 on v4

--- a/solution.py
+++ b/solution.py
@@ -106,8 +106,8 @@
     home_ref, other_ref, kernel_ref = refs[:3]
     left_first_ref, left_fwd_ref, left_back_ref, left_last_ref, right_fwd_ref, right_back_ref = refs[3:9]
     prior_ref = refs[9] if has_prior else None
-    outs = refs[9 + has_prior : -2 - last]
-    work, back = refs[-2 - last], refs[-1 - last]
+    outs = refs[9 + has_prior : -3 - last]
+    work, back, turned = refs[-3 - last], refs[-2 - last], refs[-1 - last]
     result = refs[-1] if last else outs[0]
 
     me = lax.axis_index("off")
@@ -149,6 +149,7 @@
     def first_store(block, slabs):
         for k, slab in enumerate(slabs):
             work[pl.ds((block * group + k) * pitch, grid_edge), :] = slab
+            turned[pl.ds((block * group + k) * pitch, grid_edge), :] = turn(slab, half)
 
     in_stages(grid_edge // 2 // group, first_lanes, first_rows, first_store)
 
@@ -163,8 +164,9 @@
         slabs = []
         for pair in rows_of(block):
             even, odd = (work[r, :] for r in pair)
-            top = jnp.where(in_first, even, turn(odd, half))
-            bottom = jnp.where(in_first, turn(even, half), odd)
+            turned_even, turned_odd = (turned[r, :] for r in pair)
+            top = jnp.where(in_first, even, turned_odd)
+            bottom = jnp.where(in_first, turned_even, odd)
             slabs.append(jnp.concatenate([top, bottom], axis=0))
         return rows_products(left_fwd_ref[...], slabs)
 
@@ -195,7 +197,7 @@
             dense = slabs[sources[0]]
             for k in sources[1:]:
                 dense = jnp.where(lane >= k * line - t * lanes, slabs[k], dense)
-            total = -0.25 * (dense * other[t])
+            total = dense * other[t]
             rows = pl.ds(block * tiles + t, planes, stride=row_tiles)
             for p in range(slots):
                 result[me ^ p, rows, :] = total[p * planes : (p + 1) * planes]
@@ -220,7 +222,7 @@
         left_table(basis),
         left_table(basis[:, mixed]),
         left_table(basis.T[mixed]),
-        left_table(basis.T),
+        left_table(-0.25 * basis.T),
         right_table(basis.T, grid_edge, half),
         right_table(basis, half, grid_edge),
     )
@@ -231,7 +233,7 @@
     vmem = pl.BlockSpec(memory_space=pltpu.VMEM)
     operands = [home, other, kernel, *(jnp.asarray(t) for t in tables)]
     operands += [] if prior is None else [prior]
-    scratch = [pltpu.VMEM((grid_edge // 2 * pitch, lanes), jnp.float32)] * 2
+    scratch = [pltpu.VMEM((grid_edge // 2 * pitch, lanes), jnp.float32)] * 3
     scratch += [pltpu.VMEM(whole.shape, jnp.float32)] if last else []
     return pl.pallas_call(
         functools.partial(pair_kernel, grid_edge, slots, prior is not None, last),

time: 23.2 us -> 23.1 us (level)
  no operation moved by 1% of the time
where the time goes in v5:
time: 23.1 us; the launch traced here: 22.9 us
  starting transfers between devices  9.43 us (41%)
  waiting for transfers between devices  8.15 us (35%)
  Pallas kernels  3.4 us (15%)
  other arithmetic  1.8 us (8%)
    ppermute x1, starting transfers between devices, fetch(): first = lax.ppermute(block, ('blk', 'off'), routes[0])  4.09 us
    ppermute x1, waiting for transfers between devices, scattered_sum(): arrived = lax.ppermute(far, 'off', [(g, g ^ bit) for g in range(groups)])  3.87 us
    pallas_call x2, Pallas kernels, pair_terms(): pl.pallas_call(functools.partial(pair_kernel, grid_edge, slots, prior is...  3.4 us
    ppermute x1, waiting for transfers between devices, fetch(): first = lax.ppermute(block, ('blk', 'off'), routes[0])  3.39 us
    ppermute x1, starting transfers between devices, scattered_sum(): passed_on = lax.ppermute(parts[3], 'off', to_neighbour)  2.17 us
    ppermute x1, starting transfers between devices, fetch(): second = lax.ppermute(block, ('blk', 'off'), routes[1])  1.58 us
    ppermute x1, starting transfers between devices, scattered_sum(): arrived = lax.ppermute(far, 'off', [(g, g ^ bit) for g in range(groups)])  1.51 us
    select_n x1, other arithmetic, screened_kernel(): jnp.where(squared == 0, jnp.float32(math.pi / screen_rate ** 2), screened)  1.12 us
  transfers between devices with their start and end apart: 5, of which 3 were waited for; matrix products, arithmetic and copies ran while one was open for 5% of the time, Pallas kernels for 7%

profile of v5, /device:TPU:0, one launch (start us, length us, event | category | flops | bytes accessed | tf_op | source)
XLA Modules:
  0.0 22.9 jit_solution(12735451260599878930)
XLA Ops:
  0.0 0.0 copy-start.7
  0.0 0.0 copy-start.1
  0.0 0.0 copy-start.2
  0.0 0.0 copy-start.3
  0.0 0.0 copy-start.4
  0.0 0.0 copy-start.5
  0.0 0.0 copy-start.6
  0.0 0.0 copy-start
  0.1 4.1 %collective-permute-start.1 = (bf16[1,48,2304]{2,1,0:T(8,128)(2,1)}, bf16[1,48,2304]{2,1,0:T(8,128)(2,1)S(1)}, u32[]{:S(2)}, u32[]{:S(2)}) collective-permute-start(bf16[1,48,2304]{2,1,0:T(8,128)(2,1)} %param.15), channel_id=1, source_target_pairs={{0,12},{1,17},{2,10},{3,23},{4,8},{5,21},{6,14},{7,19},{8,4},{9,25... | collective-permute-start | bytes 663560 | tf_op jit(solution)/shard_map/ppermute | solution.py:256
  4.1 1.6 %collective-permute-start = (bf16[1,48,2304]{2,1,0:T(8,128)(2,1)}, bf16[1,48,2304]{2,1,0:T(8,128)(2,1)S(1)}, u32[]{:S(2)}, u32[]{:S(2)}) collective-permute-start(bf16[1,48,2304]{2,1,0:T(8,128)(2,1)} %param.15), channel_id=1, source_target_pairs={{0,0},{1,29},{2,6},{3,27},{4,4},{5,25},{6,2},{7,31},{8,8},{9,21},{... | collective-permute-start | bytes 663560 | tf_op jit(solution)/shard_map/ppermute | solution.py:257
  5.7 0.0 copy-done.7
  5.7 1.1 %fusion.refs_2_ = f32[24,48,128]{2,1,0:T(8,128)S(1)} fusion(s32[48]{0:T(128)S(1)} %copy-done.7, s32[24,128]{1,0:T(8,128)} %constant.29.clone), kind=kLoop, calls=%fused_computation.2 | loop fusion | flops 1622016 | bytes 602304 | tf_op jit(solution)/shard_map/jit(_where)/select_n | solution.py:62
  6.9 3.4 %collective-permute-done.1 = bf16[1,48,2304]{2,1,0:T(8,128)(2,1)S(1)} collective-permute-done((bf16[1,48,2304]{2,1,0:T(8,128)(2,1)}, bf16[1,48,2304]{2,1,0:T(8,128)(2,1)S(1)}, u32[]{:S(2)}, u32[]{:S(2)}) %collective-permute-start.1) | collective-permute-done | bytes 221216 | tf_op jit(solution)/shard_map/ppermute | solution.py:256
  10.2 0.0 copy-done.1
  10.2 0.0 copy-done.2
  10.3 0.0 copy-done.3
  10.3 0.0 copy-done.4
  10.3 0.0 copy-done.5
  10.3 0.0 copy-done.6
  10.3 0.0 copy-done
  10.3 1.7 %shard_map.145.refs_9_ = f32[4,216,128]{2,1,0:T(8,128)S(1)} custom-call(bf16[48,2304]{1,0:T(8,128)(2,1)S(1)} %bitcast.4, bf16[48,2304]{1,0:T(8,128)(2,1)S(1)} %bitcast.7, f32[24,48,128]{2,1,0:T(8,128)S(1)} %fusion.refs_2_, bf16[48,144]{1,0:T(8,128)(2,1)S(1)} %copy-done.6, bf16[48,144]{1,0:T(8,128)(2,1)S(1)} %copy-done.5, bf16[48,144]{1,0:T(8,128)(2,1)S(1)} %copy-done.4, ...), custom_call_target="tpu_custom_call" | custom-call | flops 1000000000 | bytes 2000000 | tf_op jit(solution)/shard_map/pallas_call | solution.py:238
  12.0 0.0 collective-permute-done
  12.0 1.7 %shard_map.146 = (f32[1,216,128]{2,1,0:T(8,128)S(1)}, f32[1,216,128]{2,1,0:T(8,128)S(1)}, f32[1,216,128]{2,1,0:T(8,128)S(1)}, f32[1,216,128]{2,1,0:T(8,128)S(1)}) custom-call(bf16[48,2304]{1,0:T(8,128)(2,1)S(1)} %bitcast.5, bf16[48,2304]{1,0:T(8,128)(2,1)S(1)} %bitcast.6, f32[24,48,128]{2,1,0:T(8,128)S(1)} %fusion.refs_2_, bf16[48,144]{1,0:T(8,128)(2,1)S(1)} %copy-done.6, ...), custom_call_target="tpu_custom_call" | custom-call | flops 1000000000 | bytes 2000000 | tf_op jit(solution)/shard_map/pallas_call | solution.py:238
  13.7 2.2 %collective-permute-start.3 = (f32[1,216,128]{2,1,0:T(8,128)S(1)}, f32[1,216,128]{2,1,0:T(8,128)S(1)}, u32[]{:S(2)}, u32[]{:S(2)}) collective-permute-start(f32[1,216,128]{2,1,0:T(8,128)S(1)} %get-tuple-element.12), channel_id=1, source_target_pairs={{0,1},{1,0},{2,3},{3,2},{4,5},{5,4},{6,7},{7,6},{8,9},{9,8},{10,11... | collective-permute-start | bytes 331784 | tf_op jit(solution)/shard_map/ppermute | solution.py:263
  15.9 0.1 collective-permute-start.2
  16.0 0.9 %collective-permute-done.3 = f32[1,216,128]{2,1,0:T(8,128)S(1)} collective-permute-done((f32[1,216,128]{2,1,0:T(8,128)S(1)}, f32[1,216,128]{2,1,0:T(8,128)S(1)}, u32[]{:S(2)}, u32[]{:S(2)}) %collective-permute-start.3) | collective-permute-done | bytes 110624 | tf_op jit(solution)/shard_map/ppermute | solution.py:263
  16.9 1.5 %collective-permute-start.4 = (f32[1,216,128]{2,1,0:T(8,128)S(1)}, f32[1,216,128]{2,1,0:T(8,128)S(1)}, u32[]{:S(2)}, u32[]{:S(2)}) collective-permute-start(f32[1,216,128]{2,1,0:T(8,128)S(1)} %add.26), channel_id=1, source_target_pairs={{0,2},{1,3},{2,0},{3,1},{4,6},{5,7},{6,4},{7,5},{8,10},{9,11},{10,... | collective-permute-start | bytes 331784 | tf_op jit(solution)/shard_map/ppermute | solution.py:268
  18.4 0.0 collective-permute-done.2
  18.4 3.9 %collective-permute-done.4 = f32[1,216,128]{2,1,0:T(8,128)S(1)} collective-permute-done((f32[1,216,128]{2,1,0:T(8,128)S(1)}, f32[1,216,128]{2,1,0:T(8,128)S(1)}, u32[]{:S(2)}, u32[]{:S(2)}) %collective-permute-start.4) | collective-permute-done | bytes 110624 | tf_op jit(solution)/shard_map/ppermute | solution.py:268
  22.3 0.7 %add_add_fusion = f32[1,216,128]{2,1,0:T(8,128)} fusion(f32[1,216,128]{2,1,0:T(8,128)S(1)} %collective-permute-done.4, f32[1,216,128]{2,1,0:T(8,128)S(1)} %get-tuple-element.9, f32[1,216,128]{2,1,0:T(8,128)S(1)} %collective-permute-done.2), kind=kLoop, calls=%fused_computation.11 | loop fusion | flops 55296 | bytes 442368 | tf_op jit(solution)/shard_map/add | solution.py:269
  (1 shorter events, 0.0 us)
Async XLA Ops:
  0.0 5.7 %copy-start.7 = (s32[48]{0:T(128)S(1)}, s32[48]{0:T(128)}, u32[]{:S(2)}) copy-start(s32[48]{0:T(128)} %constant.30.clone) | copy-start | bytes 580
  0.0 10.2 %copy-start.1 = (bf16[256,256]{1,0:T(8,128)(2,1)S(1)}, bf16[256,256]{1,0:T(8,128)(2,1)}, u32[]{:S(2)}) copy-start(bf16[256,256]{1,0:T(8,128)(2,1)} %constant.36.clone.refs_8_) | copy-start | bytes 393220
  0.0 10.2 %copy-start.2 = (bf16[256,256]{1,0:T(8,128)(2,1)S(1)}, bf16[256,256]{1,0:T(8,128)(2,1)}, u32[]{:S(2)}) copy-start(bf16[256,256]{1,0:T(8,128)(2,1)} %constant.35.clone.refs_7_) | copy-start | bytes 393220
  0.0 10.2 %copy-start.3 = (bf16[48,144]{1,0:T(8,128)(2,1)S(1)}, bf16[48,144]{1,0:T(8,128)(2,1)}, u32[]{:S(2)}) copy-start(bf16[48,144]{1,0:T(8,128)(2,1)} %constant.34.clone.refs_6_) | copy-start | bytes 41476
  0.0 10.3 %copy-start.4 = (bf16[48,144]{1,0:T(8,128)(2,1)S(1)}, bf16[48,144]{1,0:T(8,128)(2,1)}, u32[]{:S(2)}) copy-start(bf16[48,144]{1,0:T(8,128)(2,1)} %constant.33.clone.refs_5_) | copy-start | bytes 41476
  0.0 10.3 %copy-start.5 = (bf16[48,144]{1,0:T(8,128)(2,1)S(1)}, bf16[48,144]{1,0:T(8,128)(2,1)}, u32[]{:S(2)}) copy-start(bf16[48,144]{1,0:T(8,128)(2,1)} %constant.32.clone.refs_4_) | copy-start | bytes 41476
  0.0 10.3 %copy-start.6 = (bf16[48,144]{1,0:T(8,128)(2,1)S(1)}, bf16[48,144]{1,0:T(8,128)(2,1)}, u32[]{:S(2)}) copy-start(bf16[48,144]{1,0:T(8,128)(2,1)} %constant.31.clone.refs_3_) | copy-start | bytes 41476
  0.0 10.2 %copy-start = (bf16[1,48,2304]{2,1,0:T(8,128)(2,1)S(1)}, bf16[1,48,2304]{2,1,0:T(8,128)(2,1)}, u32[]{:S(2)}) copy-start(bf16[1,48,2304]{2,1,0:T(8,128)(2,1)} %param.15) | copy-start | bytes 663556
  0.1 10.2 %collective-permute-start.1 = (bf16[1,48,2304]{2,1,0:T(8,128)(2,1)}, bf16[1,48,2304]{2,1,0:T(8,128)(2,1)S(1)}, u32[]{:S(2)}, u32[]{:S(2)}) collective-permute-start(bf16[1,48,2304]{2,1,0:T(8,128)(2,1)} %param.15), channel_id=1, source_target_pairs={{0,12},{1,17},{2,10},{3,23},{4,8},{5,21},{6,14},{7,19},{8,4},{9,25... | collective-permute-start | bytes 663560 | tf_op jit(solution)/shard_map/ppermute | solution.py:256
  4.1 7.8 %collective-permute-start = (bf16[1,48,2304]{2,1,0:T(8,128)(2,1)}, bf16[1,48,2304]{2,1,0:T(8,128)(2,1)S(1)}, u32[]{:S(2)}, u32[]{:S(2)}) collective-permute-start(bf16[1,48,2304]{2,1,0:T(8,128)(2,1)} %param.15), channel_id=1, source_target_pairs={{0,0},{1,29},{2,6},{3,27},{4,4},{5,25},{6,2},{7,31},{8,8},{9,21},{... | collective-permute-start | bytes 663560 | tf_op jit(solution)/shard_map/ppermute | solution.py:257
  13.7 3.1 %collective-permute-start.3 = (f32[1,216,128]{2,1,0:T(8,128)S(1)}, f32[1,216,128]{2,1,0:T(8,128)S(1)}, u32[]{:S(2)}, u32[]{:S(2)}) collective-permute-start(f32[1,216,128]{2,1,0:T(8,128)S(1)} %get-tuple-element.12), channel_id=1, source_target_pairs={{0,1},{1,0},{2,3},{3,2},{4,5},{5,4},{6,7},{7,6},{8,9},{9,8},{10,11... | collective-permute-start | bytes 331784 | tf_op jit(solution)/shard_map/ppermute | solution.py:263
  15.9 2.5 %collective-permute-start.2 = (f32[1,216,128]{2,1,0:T(8,128)S(1)}, f32[1,216,128]{2,1,0:T(8,128)S(1)}, u32[]{:S(2)}, u32[]{:S(2)}) collective-permute-start(f32[1,216,128]{2,1,0:T(8,128)S(1)} %get-tuple-element.10), channel_id=1, source_target_pairs={{0,1},{1,0},{2,3},{3,2},{4,5},{5,4},{6,7},{7,6},{8,9},{9,8},{10,11... | collective-permute-start | bytes 331784 | tf_op jit(solution)/shard_map/ppermute | solution.py:264
  16.9 5.4 %collective-permute-start.4 = (f32[1,216,128]{2,1,0:T(8,128)S(1)}, f32[1,216,128]{2,1,0:T(8,128)S(1)}, u32[]{:S(2)}, u32[]{:S(2)}) collective-permute-start(f32[1,216,128]{2,1,0:T(8,128)S(1)} %add.26), channel_id=1, source_target_pairs={{0,2},{1,3},{2,0},{3,1},{4,6},{5,7},{6,4},{7,5},{8,10},{9,11},{10,... | collective-permute-start | bytes 331784 | tf_op jit(solution)/shard_map/ppermute | solution.py:268
